TPU v7x, 32 devices: a whole 2x2x4 slice. The times are simulated.
32 devices in a mesh: ctx: 8 (over y, x, core), fsdp: 4 (over z).
Axes of the slice: x: 2, y: 2, z: 4, core: 2. Of those that a mesh axis runs over, the one named last changes fastest.
Arguments:
- block_input: bfloat16 [4, 1024, 2048], P('fsdp', 'ctx'), may hold values from -6 to 6
- output_grad: bfloat16 [4, 1024, 2048], P('fsdp', 'ctx'), may hold values from -6 to 6
- segment: int32 [4, 1024], P('fsdp'), may hold values from 0 to 3, never falling along the last dimension, each value on 1 to 512 neighbouring positions
- slots: int32 [16], replicated, may hold values from 0 to 15, each once
- ln_gain: bfloat16 [2048], P(('ctx', 'fsdp')), may hold values from 0.5 to 1.5
- ln_bias: bfloat16 [2048], P(('ctx', 'fsdp')), may hold values from -2 to 2
- qkv_w: bfloat16 [2048, 6144], P(('ctx', 'fsdp')), may hold values from -1 to 1
- qkv_b: bfloat16 [6144], P(('ctx', 'fsdp')), may hold values from -0.59765625 to 0.59765625
- dense_w: bfloat16 [2048, 2048], P(('ctx', 'fsdp')), may hold values from -0.5 to 0.5
- dense_b: bfloat16 [2048], P(('ctx', 'fsdp')), may hold values from -2 to 2
- fc1_w: bfloat16 [2048, 8192], P(('ctx', 'fsdp')), may hold values from -0.125 to 0.125
- fc1_b: bfloat16 [8192], P(('ctx', 'fsdp')), may hold values from -2 to 2
- fc2_w: bfloat16 [8192, 2048], P(('ctx', 'fsdp')), may hold values from -0.0625 to 0.0625
- fc2_b: bfloat16 [2048], P(('ctx', 'fsdp')), may hold values from -2 to 2
Outputs:
- block_output: bfloat16 [4, 1024, 2048], P('fsdp', 'ctx')
- input_grad: float32 [4, 1024, 2048], P('fsdp', 'ctx')
- d_ln_gain: float32 [2048], P(('ctx', 'fsdp'))
- d_ln_bias: float32 [2048], P(('ctx', 'fsdp'))
- d_qkv_w: float32 [2048, 6144], P(('ctx', 'fsdp'))
- d_qkv_b: float32 [6144], P(('ctx', 'fsdp'))
- d_dense_w: float32 [2048, 2048], P(('ctx', 'fsdp'))
- d_dense_b: float32 [2048], P(('ctx', 'fsdp'))
- d_fc1_w: float32 [2048, 8192], P(('ctx', 'fsdp'))
- d_fc1_b: float32 [8192], P(('ctx', 'fsdp'))
- d_fc2_w: float32 [8192, 2048], P(('ctx', 'fsdp'))
- d_fc2_b: float32 [2048], P(('ctx', 'fsdp'))
Inputs may be any that keep to these rules, and one draw needn't show every extreme that they name: `segment`: ids never fall along positions; each of the 4 documents of a sequence spans 1 to 512 positions, one exactly that many. `slots`: every stretch number appears exactly once.
All inputs are finite; a program needn't handle non-finite values.
Results may differ from a plain program's by a relative error of at most 0.014.
Values may be sent and summed in bfloat16 or wider, within the bound.
A program may use at most 384 MiB of HBM per device.

v0:
```python
import math

import jax
import jax.numpy as jnp
from jax import lax
from jax.experimental import pallas as pl
from jax.experimental.pallas import tpu as pltpu
from jax.sharding import PartitionSpec as P

HEADS = 32
ROT = 32


EPS = 1e-05
GELU_C = math.sqrt(2.0 / math.pi)
NEG = -1e30


def shifted(block, axis, distance):
    devices = range(lax.axis_size(axis))
    route = [((i - distance) % len(devices), i) for i in devices]
    return lax.ppermute(block, axis, route)


def gelu_pair(upper):
    inner = GELU_C * (upper + 0.044715 * upper * upper * upper)
    tanh_val = jnp.tanh(inner)
    value = 0.5 * upper * (1.0 + tanh_val)
    slope = 0.5 * (1.0 + tanh_val) + 0.5 * upper * (1.0 - tanh_val * tanh_val) * GELU_C * (
        1.0 + 3.0 * 0.044715 * upper * upper
    )
    return (value, slope)


def rotary_tables(positions):
    half = ROT // 2
    freqs = jnp.exp(-(2.0 * jnp.arange(half, dtype=jnp.float32) / ROT) * math.log(10000.0))
    angles = positions.astype(jnp.float32)[:, None] * freqs[None, :]
    return (jnp.cos(angles)[:, None, :], jnp.sin(angles)[:, None, :])


def rotate(tensor, cosine, sine, sign):
    half = ROT // 2
    first = tensor[..., :half]
    second = tensor[..., half:ROT]
    new_first = first * cosine - sign * second * sine
    new_second = second * cosine + sign * first * sine
    return jnp.concatenate([new_first, new_second, tensor[..., ROT:]], axis=-1)


def contract_rows(left, right):
    return lax.dot_general(
        left, right, (((0,), (0,)), ((), ())), preferred_element_type=jnp.float32
    )


def contract_cols(left, right):
    return lax.dot_general(
        left, right, (((1,), (1,)), ((), ())), preferred_element_type=jnp.float32
    )


def own_columns(matrix, cycle_size, shard_count, member):
    count = matrix.shape[0]
    piece_width = matrix.shape[1] // (cycle_size * shard_count)
    parted = matrix.reshape(count, cycle_size, shard_count, piece_width)
    return lax.dynamic_slice_in_dim(parted, member, 1, 2).reshape(count, cycle_size * piece_width)


def per_device(
    block_input,
    output_grad,
    segment,
    slots,
    ln_gain,
    ln_bias,
    qkv_w,
    qkv_b,
    dense_w,
    dense_b,
    fc1_w,
    fc1_b,
    fc2_w,
    fc2_b,
):
    cycle_size = lax.axis_size("ctx")
    index = lax.axis_index("ctx")
    shard_count = lax.axis_size("fsdp")
    member = lax.axis_index("fsdp")
    tokens = block_input.shape[1]
    width = block_input.shape[2]
    stretch = tokens // 2
    heads = HEADS
    head_dim = width // heads
    scale = head_dim ** (-0.5)
    seg_row = segment[0]
    slot_ids = jnp.arange(2 * cycle_size, dtype=jnp.int32)

    def positions(start, count):
        rows = start + jnp.arange(count, dtype=jnp.int32)
        slot = rows // stretch
        owner = jnp.sum(jnp.where(slot[:, None] == slot_ids[None, :], slots[None, :], 0), axis=1)
        return owner * stretch + rows % stretch

    qpos = positions(index * tokens, tokens)
    qdoc = jnp.take(seg_row, qpos)
    cosine, sine = rotary_tables(qpos)
    gain_all, norm_bias_every, w_qkv, b_qkv, w_up, b_up = (
        lax.all_gather(ln_gain, ("ctx", "fsdp"), axis=0, tiled=True),
        lax.all_gather(ln_bias, ("ctx", "fsdp"), axis=0, tiled=True),
        lax.all_gather(qkv_w, ("ctx", "fsdp"), axis=0, tiled=True),
        lax.all_gather(qkv_b, ("ctx", "fsdp"), axis=0, tiled=True),
        lax.all_gather(fc1_w, ("ctx", "fsdp"), axis=0, tiled=True),
        lax.all_gather(fc1_b, ("ctx", "fsdp"), axis=0, tiled=True),
    )
    xf = block_input[0].astype(jnp.float32)
    row_mean = jnp.mean(xf, axis=-1, keepdims=True)
    centered_input = xf - row_mean
    inverse_deviation = lax.rsqrt(
        jnp.mean(centered_input * centered_input, axis=-1, keepdims=True) + EPS
    )
    standardized_input = centered_input * inverse_deviation
    gain_float = gain_all.astype(jnp.float32)
    normed_rows = (standardized_input * gain_float + norm_bias_every.astype(jnp.float32)).astype(
        jnp.bfloat16
    )
    proj = jnp.dot(normed_rows, w_qkv, preferred_element_type=jnp.float32) + b_qkv.astype(
        jnp.float32
    )
    query = rotate(proj[:, :width].reshape(tokens, heads, head_dim), cosine, sine, 1.0).astype(
        jnp.bfloat16
    )
    keys = rotate(
        proj[:, width : 2 * width].reshape(tokens, heads, head_dim), cosine, sine, 1.0
    ).astype(jnp.bfloat16)
    keys_flat = keys.reshape(tokens, width)
    values = proj[:, 2 * width :].astype(jnp.bfloat16)
    acc = jnp.zeros((tokens, heads, head_dim), jnp.float32)
    top = jnp.full((heads, tokens), NEG, jnp.float32)
    key_piece = lax.all_gather(keys_flat, "ctx", axis=0, tiled=True)
    value_piece = lax.all_gather(values, "ctx", axis=0, tiled=True)
    count = key_piece.shape[0]
    kpos = positions(jnp.int32(0), count)
    kdoc = jnp.take(seg_row, kpos)
    mask = ((kpos[None, :] <= qpos[:, None]) & (kdoc[None, :] == qdoc[:, None]))[None]
    scores = (
        jnp.einsum(
            "qhd,khd->hqk",
            query,
            key_piece.reshape(count, heads, head_dim),
            preferred_element_type=jnp.float32,
        )
        * scale
    )
    scores = jnp.where(mask, scores, NEG)
    new_top = jnp.maximum(top, jnp.max(scores, axis=-1))
    factor = jnp.exp(top - new_top)
    expo = jnp.where(mask, jnp.exp(scores - new_top[..., None]), 0.0)
    total = jnp.sum(expo, axis=-1)
    part_sum = jnp.einsum(
        "hqk,khd->qhd",
        expo.astype(jnp.bfloat16),
        value_piece.reshape(count, heads, head_dim),
        preferred_element_type=jnp.float32,
    )
    acc = acc * factor.T[:, :, None] + part_sum
    acc, top, total = (acc, new_top, total)
    attn_heads = (acc / total.T[:, :, None]).astype(jnp.bfloat16)
    lse = top + jnp.log(total)
    attn = attn_heads.reshape(tokens, width)
    w_dense, b_dense, w_down, b_down = (
        lax.all_gather(dense_w, ("ctx", "fsdp"), axis=0, tiled=True),
        lax.all_gather(dense_b, ("ctx", "fsdp"), axis=0, tiled=True),
        lax.all_gather(fc2_w, ("ctx", "fsdp"), axis=0, tiled=True),
        lax.all_gather(fc2_b, ("ctx", "fsdp"), axis=0, tiled=True),
    )
    upper = jnp.dot(normed_rows, w_up, preferred_element_type=jnp.float32) + b_up.astype(
        jnp.float32
    )
    act_f, slope = gelu_pair(upper)
    act = act_f.astype(jnp.bfloat16)
    y_rows = (
        xf
        + jnp.dot(attn, w_dense, preferred_element_type=jnp.float32)
        + b_dense.astype(jnp.float32)
    )
    y_rows = (
        y_rows
        + jnp.dot(act, w_down, preferred_element_type=jnp.float32)
        + b_down.astype(jnp.float32)
    )
    grad_rows = output_grad[0]
    gradient_float = grad_rows.astype(jnp.float32)
    group_attn, group_act, group_grad = (
        lax.all_gather(attn, "fsdp", axis=0, tiled=True),
        lax.all_gather(act, "fsdp", axis=0, tiled=True),
        lax.all_gather(grad_rows, "fsdp", axis=0, tiled=True),
    )
    group_bias = jnp.sum(group_grad.astype(jnp.float32), axis=0)
    own_bias = own_columns(group_bias[None], cycle_size, shard_count, member)[0]
    dense_part = contract_rows(own_columns(group_attn, cycle_size, shard_count, member), group_grad)
    down_part = contract_rows(own_columns(group_act, cycle_size, shard_count, member), group_grad)
    g_dense_w, g_dense_b, g_fc2_w, g_fc2_b = (
        lax.psum_scatter(
            dense_part.astype(jnp.bfloat16), "ctx", scatter_dimension=0, tiled=True
        ).astype(jnp.float32),
        lax.psum_scatter(
            own_bias.astype(jnp.bfloat16), "ctx", scatter_dimension=0, tiled=True
        ).astype(jnp.float32),
        lax.psum_scatter(
            down_part.astype(jnp.bfloat16), "ctx", scatter_dimension=0, tiled=True
        ).astype(jnp.float32),
        lax.psum_scatter(
            own_bias.astype(jnp.bfloat16), "ctx", scatter_dimension=0, tiled=True
        ).astype(jnp.float32),
    )
    dup = contract_cols(grad_rows, w_down) * slope
    up_bias_grad = jnp.sum(dup, axis=0)
    dup_b = dup.astype(jnp.bfloat16)
    dattn = contract_cols(grad_rows, w_dense).astype(jnp.bfloat16).reshape(tokens, heads, head_dim)
    delta = jnp.sum(dattn.astype(jnp.float32) * attn_heads.astype(jnp.float32), axis=-1).T

    def cycle_step(step, carry):
        key_cur, value_cur, dkey_acc, dvalue_acc, dquery_acc = carry
        anchor = (index - step + cycle_size) % cycle_size
        kpos = positions(anchor * tokens, tokens)
        kdoc = jnp.take(seg_row, kpos)
        mask = ((kpos[None, :] <= qpos[:, None]) & (kdoc[None, :] == qdoc[:, None]))[None]
        key_heads = key_cur.reshape(tokens, heads, head_dim)
        scores = (
            jnp.einsum("qhd,khd->hqk", query, key_heads, preferred_element_type=jnp.float32) * scale
        )
        probs = jnp.where(mask, jnp.exp(jnp.where(mask, scores, NEG) - lse[..., None]), 0.0)
        dvalue_acc = dvalue_acc + jnp.einsum(
            "hqk,qhd->khd", probs.astype(jnp.bfloat16), dattn, preferred_element_type=jnp.float32
        ).reshape(tokens, width)
        dprob = jnp.einsum(
            "qhd,khd->hqk",
            dattn,
            value_cur.reshape(tokens, heads, head_dim),
            preferred_element_type=jnp.float32,
        )
        dscore = (probs * (dprob - delta[..., None]) * scale).astype(jnp.bfloat16)
        dquery_acc = dquery_acc + jnp.einsum(
            "hqk,khd->qhd", dscore, key_heads, preferred_element_type=jnp.float32
        )
        dkey_acc = dkey_acc + jnp.einsum(
            "hqk,qhd->khd", dscore, query, preferred_element_type=jnp.float32
        ).reshape(tokens, width)
        key_cur, value_cur = shifted((key_cur, value_cur), "ctx", 1)
        dkey_acc, dvalue_acc = (
            shifted(dkey_acc.astype(jnp.bfloat16), "ctx", 1).astype(dkey_acc.dtype),
            shifted(dvalue_acc.astype(jnp.bfloat16), "ctx", 1).astype(dvalue_acc.dtype),
        )
        return (key_cur, value_cur, dkey_acc, dvalue_acc, dquery_acc)

    flat_zero = jnp.zeros((tokens, width), jnp.float32)
    cycle_init = (
        keys_flat,
        values,
        flat_zero,
        flat_zero,
        jnp.zeros((tokens, heads, head_dim), jnp.float32),
    )
    cycle_out = lax.fori_loop(0, cycle_size, cycle_step, cycle_init)
    dkey_sum, dvalue_sum, dquery_sum = (cycle_out[2], cycle_out[3], cycle_out[4])
    dquery = rotate(dquery_sum, cosine, sine, -1.0).reshape(tokens, width)
    dkey = rotate(dkey_sum.reshape(tokens, heads, head_dim), cosine, sine, -1.0).reshape(
        tokens, width
    )
    dproj = jnp.concatenate([dquery, dkey, dvalue_sum], axis=1)
    qkv_bias_grad = jnp.sum(dproj, axis=0)
    dproj_b = dproj.astype(jnp.bfloat16)
    normed_input_grad = contract_cols(dproj_b, w_qkv) + contract_cols(dup_b, w_up)
    gain_gradient = jnp.sum(normed_input_grad * standardized_input, axis=0)
    lnb_grad = jnp.sum(normed_input_grad, axis=0)
    scaled_rows = normed_input_grad * gain_float
    dx_rows = gradient_float + inverse_deviation * (
        scaled_rows
        - jnp.mean(scaled_rows, axis=-1, keepdims=True)
        - standardized_input * jnp.mean(scaled_rows * standardized_input, axis=-1, keepdims=True)
    )
    group_normed, group_dproj, group_dup = (
        lax.all_gather(normed_rows, "fsdp", axis=0, tiled=True),
        lax.all_gather(dproj_b, "fsdp", axis=0, tiled=True),
        lax.all_gather(dup_b, "fsdp", axis=0, tiled=True),
    )
    own_normed = own_columns(group_normed, cycle_size, shard_count, member)
    g_qkv_w, g_fc1_w = (
        lax.psum_scatter(
            contract_rows(own_normed, group_dproj).astype(jnp.bfloat16),
            "ctx",
            scatter_dimension=0,
            tiled=True,
        ).astype(jnp.float32),
        lax.psum_scatter(
            contract_rows(own_normed, group_dup).astype(jnp.bfloat16),
            "ctx",
            scatter_dimension=0,
            tiled=True,
        ).astype(jnp.float32),
    )
    layer_gain_grad, g_lnb, g_qkv_b, g_fc1_b = (
        lax.psum_scatter(gain_gradient, ("ctx", "fsdp"), scatter_dimension=0, tiled=True),
        lax.psum_scatter(lnb_grad, ("ctx", "fsdp"), scatter_dimension=0, tiled=True),
        lax.psum_scatter(qkv_bias_grad, ("ctx", "fsdp"), scatter_dimension=0, tiled=True),
        lax.psum_scatter(up_bias_grad, ("ctx", "fsdp"), scatter_dimension=0, tiled=True),
    )
    return (
        y_rows.astype(jnp.bfloat16)[None],
        dx_rows[None],
        layer_gain_grad,
        g_lnb,
        g_qkv_w,
        g_qkv_b,
        g_dense_w,
        g_dense_b,
        g_fc1_w,
        g_fc1_b,
        g_fc2_w,
        g_fc2_b,
    )


BF = jnp.bfloat16
F32 = jnp.float32
MESH = pl.DeviceIdType.MESH
HBM = pl.BlockSpec(memory_space=pl.ANY)
VM = pl.BlockSpec(memory_space=pltpu.VMEM)
DMA = pltpu.SemaphoreType.DMA
VLIM = 60 * 1024 * 1024


def place():
    ctx, z = lax.axis_index("ctx"), lax.axis_index("fsdp")
    return ctx, lax.div(ctx, 4), lax.rem(lax.div(ctx, 2), 2), lax.rem(ctx, 2), z


class Net:
    def __init__(self):
        self.ctx, self.y, self.x, self.c, self.z = place()
        self.yb, self.xb, self.cb = 1 - self.y, 1 - self.x, 1 - self.c
        self.m = self.y * 4 + self.z
        self.g = self.x * 2 + self.c
        self.to_y = {"ctx": self.ctx + 4 * (1 - 2 * self.y), "fsdp": self.z}
        self.to_x = {"ctx": self.ctx + 2 * (1 - 2 * self.x), "fsdp": self.z}
        self.to_c = {"ctx": self.ctx + 1 - 2 * self.c, "fsdp": self.z}
        self.up = {"ctx": self.ctx, "fsdp": self.z + 1}
        self.dn = {"ctx": self.ctx, "fsdp": self.z - 1}
        self.sent = []

    def member(self, q):
        flip, step = q // 4, q % 4
        z = lax.rem(self.z + step, 4)
        yy = self.yb if flip else self.y
        return {"ctx": self.ctx + flip * 4 * (1 - 2 * self.y), "fsdp": z}, yy, z

    def source(self, q):
        flip, step = q // 4, q % 4
        return (self.yb if flip else self.y), lax.rem(self.z + 4 - step, 4)

    def barrier(self, more=()):
        sem = pltpu.get_barrier_semaphore()
        peers = [self.member(q)[0] for q in range(1, 8)] + [self.to_x, self.to_c, *more]
        for peer in peers:
            pl.semaphore_signal(sem, inc=1, device_id=peer, device_id_type=MESH)
        pl.semaphore_wait(sem, len(peers))

    def go(self, copy, when=None):
        if when is None:
            copy.start()
        else:
            pl.when(when)(copy.start)
        self.sent.append((copy, when))

    def drain(self):
        for copy, when in self.sent:
            if when is None:
                copy.wait_send()
            else:
                pl.when(when)(copy.wait_send)


def remote(src, dst, send, recv, to):
    return pltpu.make_async_remote_copy(
        src_ref=src, dst_ref=dst, send_sem=send, recv_sem=recv, device_id=to, device_id_type=MESH
    )


def arrive(like, recv):
    pltpu.make_async_copy(like, like, recv).wait()


def head_tiles(src, dst, rows):
    qkv, ff = src
    low = lanes_of((rows, 128)) < 64

    def tile(base, h):
        t = 128 * (h // 2)
        return qkv[:, base + t : base + t + 128].astype(F32)

    def join(a, b, odd):
        if odd:
            return jnp.where(low, pltpu.roll(a, 64, 1), b).astype(BF)
        return jnp.where(low, a, pltpu.roll(b, 64, 1)).astype(BF)

    for mm in range(8):
        first = (mm // 4) * 16 + mm % 4
        odd = first % 2
        for g in range(4):
            h = first + 4 * g
            dst(mm, 128 * g, join(tile(0, h), tile(2048, h), odd))
            dst(mm, 768 + 256 * g, ff[:, 256 * h : 256 * h + 256])
        for k in range(2):
            h = first + 8 * k
            dst(mm, 512 + 128 * k, join(tile(4096, h), tile(4096, h + 4), odd))


def gather_kernel(x, dy, docs, qkv, ff, qb, fb, small, fc2, dense, cos, sin,
                  xg, dg, docg, normed_o, act_o, dup_o, wc_o, w2_o, heads, dsum, cst,
                  xv, dv, wc, w2g, eg, ws, es, nrm, act, dup, hs,
                  loc, us, ur, ds_, dr, ys, yr, as_, ar, es_, er,
                  wxs, wxr, wks, wkr, exs, exr, eks, ekr, fxs, fxr, fks, fkr, hss, hsr, hl, wb):
    n = Net()
    far = {"ctx": n.ctx + 2 * (1 - 2 * n.x) + 1 - 2 * n.c, "fsdp": n.z}
    n.barrier(more=(far,))

    def wrow(yy, xx, cc, zz):
        return wc.at[pl.ds(pl.multiple_of((yy * 16 + xx * 8 + cc * 4 + zz) * 64, 64), 64)]

    def wide(gg):
        return w2g.at[pl.ds(pl.multiple_of(gg * 256, 256), 256)]

    def thin(gg):
        return w2g.at[pl.ds(pl.multiple_of(1024 + gg * 64, 64), 64)]

    def shard(yy, zz, p):
        mm = yy * 4 + zz
        if p == 2:
            return docg.at[mm]
        return (xv, dv)[p].at[pl.ds(pl.multiple_of(mm * 128, 128), 128)]

    mine = (x, dy, docs)
    parts = (0, 1, 2)

    def tokens(p):
        n.go(remote(mine[p], shard(n.y, n.z, p), us.at[p, 0], ur.at[p, 0], n.up), n.z < 3)
        n.go(remote(mine[p], shard(n.y, n.z, p), ds_.at[p, 0], dr.at[p, 0], n.dn), n.z > 0)
        n.go(remote(mine[p], shard(n.y, n.z, p), ys.at[p, 0], yr.at[p, n.z], n.to_y))

    tokens(0)
    rows2 = ((fc2, wide), (dense, thin))
    for k, (ref, part) in enumerate(rows2):
        n.go(remote(ref, part(n.g), fxs.at[k], fxr.at[k], n.to_x))
        n.go(remote(ref, part(n.g), fks.at[k], fkr.at[k], n.to_c))

    def put_w(mm, col, value):
        ws[mm, :, col : col + value.shape[1]] = value

    def put_e(mm, col, value):
        es[mm, 0:1, col : col + value.shape[1]] = value[0:1]

    for mm in range(8):
        es[mm] = small[...]
    head_tiles((qkv, ff), put_w, 64)
    head_tiles((qb, fb), put_e, 8)
    for q in (4, 1, 3, 5, 7, 2, 6):
        to, yy, zz = n.member(q)
        n.go(remote(es.at[yy * 4 + zz], eg.at[n.g * 8 + n.m], es_.at[q], er.at[q], to))
        n.go(remote(ws.at[yy * 4 + zz], wrow(n.y, n.x, n.c, n.z), as_.at[q], ar.at[q], to))
    own = ws.at[n.m]
    n.go(remote(own, wrow(n.y, n.x, n.c, n.z), wxs.at[0], wxr.at[0], n.to_x))
    n.go(remote(own, wrow(n.y, n.x, n.c, n.z), wks.at[0], wkr.at[0], n.to_c))
    tokens(1)
    tokens(2)
    local = [
        pltpu.make_async_copy(x, shard(n.y, n.z, 0), loc.at[0]),
        pltpu.make_async_copy(dy, shard(n.y, n.z, 1), loc.at[1]),
        pltpu.make_async_copy(docs, shard(n.y, n.z, 2), loc.at[2]),
        pltpu.make_async_copy(own, wrow(n.y, n.x, n.c, n.z), loc.at[3]),
        pltpu.make_async_copy(es.at[n.m], eg.at[n.g * 8 + n.m], loc.at[4]),
        pltpu.make_async_copy(fc2, wide(n.g), loc.at[5]),
        pltpu.make_async_copy(dense, thin(n.g), loc.at[6]),
    ]
    for copy in local:
        copy.start()

    def line(d, ps):
        below, above = n.z >= d, n.z + d <= 3
        for p in ps:
            for there, zz, recv, send, nxt, more, to in (
                (below, n.z - d, ur, us, ur, n.z < 3, n.up),
                (above, n.z + d, dr, ds_, dr, n.z > 0, n.dn),
            ):
                block = shard(n.y, zz, p)

                @pl.when(there)
                def _():
                    arrive(block, recv.at[p, d - 1])

                if d < 3:
                    n.go(remote(block, block, send.at[p, d], nxt.at[p, d], to), there & more)
                slot = d if to is n.up else d + 3
                n.go(remote(block, block, ys.at[p, slot], yr.at[p, zz], n.to_y), there)

    def pieces(qs):
        for q in qs:
            yy, zz = n.source(q)
            block = wrow(yy, n.x, n.c, zz)
            arrive(block, ar.at[q])
            n.go(remote(block, block, wxs.at[q], wxr.at[q], n.to_x))
            n.go(remote(block, block, wks.at[q], wkr.at[q], n.to_c))

    def relay(qs):
        for q in qs:
            yy, zz = n.source(q)
            block = wrow(yy, n.xb, n.c, zz)
            arrive(block, wxr.at[q])
            n.go(remote(block, block, wks.at[8 + q], wkr.at[8 + q], n.to_c))

    line(1, (0,))
    pieces((4, 1, 3))
    line(1, (1, 2))
    pieces((5, 7, 2, 6))
    for q in range(1, 8):
        yy, zz = n.source(q)
        arrive(eg.at[n.g * 8 + yy * 4 + zz], er.at[q])
    local[4].wait()
    these = eg.at[pl.ds(n.g * 8, 8)]
    n.go(remote(these, these, exs.at[0], exr.at[0], n.to_x))
    n.go(remote(these, these, eks.at[0], ekr.at[0], n.to_c))
    line(2, parts)
    gx = n.xb * 2 + n.c
    for k, (ref, part) in enumerate(rows2):
        arrive(part(gx), fxr.at[k])
        n.go(remote(part(gx), part(gx), fks.at[2 + k], fkr.at[2 + k], n.to_c))
    theirs = eg.at[pl.ds(gx * 8, 8)]
    relay((0, 4, 1, 3, 5, 7, 2, 6))
    arrive(theirs, exr.at[0])
    n.go(remote(theirs, theirs, eks.at[1], ekr.at[1], n.to_c))
    for q in range(8):
        yy, zz = n.source(q)
        arrive(wrow(yy, n.x, n.cb, zz), wkr.at[q])
        arrive(wrow(yy, n.xb, n.cb, zz), wkr.at[8 + q])
    for k in range(2):
        gg = 2 * (n.xb if k else n.x) + n.cb
        arrive(eg.at[pl.ds(gg * 8, 8)], ekr.at[k])
        for j, (ref, part) in enumerate(rows2):
            arrive(part(gg), fkr.at[2 * k + j])
    for k in (0, 1, 2, 3, 5, 6):
        local[k].wait()
    out_w = [pltpu.make_async_copy(wc, wc_o, wb.at[0]), pltpu.make_async_copy(w2g, w2_o, wb.at[1])]
    for copy in out_w:
        copy.start()

    def add_ext(i, t):
        return t + eg[i].astype(F32)

    ext = lax.fori_loop(0, 32, add_ext, jnp.zeros((8, 1792), F32))
    cst[0:1, 0:1792], cst[0:1, 1792:2048] = ext[1:2], ext[5:6, 0:256]
    cst[1:2, 0:1792], cst[1:2, 1792:2048] = ext[2:3], ext[5:6, 256:512]
    cst[2:3, 0:1792], cst[2:3, 1792:2048] = ext[3:4] + ext[4:5], ext[5:6, 512:768] + ext[5:6, 768:1024]
    cst[3:4, 0:1792], cst[3:4, 1792:2048] = ext[0:1], jnp.zeros((1, 256), F32)
    cst[4:8, :] = jnp.zeros((4, 2048), F32)
    dsum[...] = jnp.zeros_like(dsum)
    z0 = lax.div(n.z, 2)
    half = lanes_of((256, 128)) < 64

    def rows_of(j):
        yy = n.y + lax.rem(j, 2) * (1 - 2 * n.y)
        zp = z0 + lax.div(j, 2) * (1 - 2 * z0)
        return yy, zp, pl.ds(pl.multiple_of((yy * 4 + 2 * zp) * 128, 256), 256)

    def sends(j):
        yy, zp, rows = rows_of(j)
        return [
            remote(hs.at[gg, rows], heads.at[n.g, rows], hss.at[j, k], hsr.at[j, k], to)
            for k, (to, gg) in enumerate(((far, 2 * n.xb + n.cb), (n.to_x, 2 * n.xb + n.c), (n.to_c, 2 * n.x + n.cb)))
        ]

    def keeps(j):
        yy, zp, rows = rows_of(j)
        return [
            pltpu.make_async_copy(hs.at[n.g, rows], heads.at[n.g, rows], hl.at[j, 0]),
            pltpu.make_async_copy(nrm.at[rows], normed_o.at[rows], hl.at[j, 1]),
            pltpu.make_async_copy(act.at[rows], act_o.at[rows], hl.at[j, 2]),
            pltpu.make_async_copy(dup.at[rows], dup_o.at[rows], hl.at[j, 3]),
            pltpu.make_async_copy(xv.at[rows], xg.at[rows], hl.at[j, 4]),
            pltpu.make_async_copy(dv.at[rows], dg.at[rows], hl.at[j, 5]),
        ]

    def pair(j, carry):
        yy, zp, rows = rows_of(j)
        base = (yy * 4 + 2 * zp) * 128

        @pl.when(lax.rem(j, 2) == 1)
        def _():
            for k in range(2):
                for p in parts:
                    arrive(shard(yy, 2 * zp + k, p), yr.at[p, 2 * zp + k])

        def norm(i, c):
            sl = pl.ds(pl.multiple_of(base + 32 * i, 32), 32)
            xf = xv[sl, :].astype(F32)
            cen = xf - jnp.mean(xf, axis=-1, keepdims=True)
            rstd = lax.rsqrt(jnp.mean(cen * cen, axis=-1, keepdims=True) + EPS)
            nrm[sl, :] = (cen * rstd * cst[0:1, :] + cst[1:2, :]).astype(BF)
            return c

        lax.fori_loop(0, 8, norm, 0)
        table = pl.ds(pl.multiple_of(yy * 128, 128), 128)
        cosv = jnp.concatenate([cos[table, :]] * 2, axis=0)
        sinv = jnp.concatenate([sin[table, :]] * 2, axis=0)
        for k in range(2):
            t2 = jnp.dot(nrm[rows, :], wc[:, 256 * k : 256 * k + 256], preferred_element_type=F32)
            t2 = t2 + cst[3:4, 256 * k : 256 * k + 256]
            for i in range(2):
                t = t2[:, 128 * i : 128 * i + 128]
                hs[2 * k + i, rows, 0:128] = (t * cosv + partner(t) * sinv).astype(BF)
        v4 = jnp.dot(nrm[rows, :], wc[:, 512:768], preferred_element_type=F32) + cst[3:4, 512:768]
        d4 = dot_nt(dv[rows, :], w2g[1024:1280, :])
        for g in range(4):
            v, d = (t[:, 128 * (g // 2) : 128 * (g // 2) + 128] for t in (v4, d4))
            if g % 2 == 0:
                vd = jnp.where(half, v, pltpu.roll(d, 64, 1))
            else:
                vd = jnp.where(half, pltpu.roll(v, 64, 1), d)
            hs[g, rows, 128:256] = vd.astype(BF)
        for copy in sends(j):
            copy.start()
        for k in range(4):
            cols, wcols = slice(256 * k, 256 * k + 256), slice(768 + 256 * k, 1024 + 256 * k)
            up = jnp.dot(nrm[rows, :], wc[:, wcols], preferred_element_type=F32) + cst[3:4, wcols]
            a, slope = gelu_pair(up)
            act[rows, cols] = a.astype(BF)
            du = dot_nt(dv[rows, :], w2g[cols, :]) * slope
            dup[rows, cols] = du.astype(BF)
            dsum[:, cols] += jnp.broadcast_to(jnp.sum(du, axis=0, keepdims=True), (8, 256))
        for copy in keeps(j):
            copy.start()
        return carry

    lax.fori_loop(0, 2, pair, 0)
    line(3, parts)
    lax.fori_loop(2, 4, pair, 0)
    for j in range(4):
        for copy in sends(j):
            copy.wait()
        for copy in keeps(j):
            copy.wait()
    for copy in out_w:
        copy.wait()
    n.drain()


def gather_all(x, dy, docs, qkv, ff, qb, fb, small, fc2, dense, cos, sin):
    sd = jax.ShapeDtypeStruct
    V = pltpu.VMEM
    return pl.pallas_call(
        gather_kernel,
        name="gather_all",
        out_shape=(sd((1024, 2048), BF), sd((1024, 2048), BF), sd((8, 8, 1024), BF), sd((1024, 2048), BF),
                   sd((1024, 1024), BF), sd((1024, 1024), BF), sd((2048, 1792), BF), sd((1280, 2048), BF),
                   sd((4, 1024, 256), BF), sd((8, 1024), F32), sd((8, 2048), F32)),
        in_specs=[VM] * 12,
        out_specs=(HBM, HBM, VM, HBM, HBM, HBM, HBM, HBM, HBM, VM, VM),
        scratch_shapes=[V((1024, 2048), BF), V((1024, 2048), BF), V((2048, 1792), BF), V((1280, 2048), BF),
                        V((32, 8, 1792), BF), V((8, 64, 1792), BF), V((8, 8, 1792), BF),
                        V((1024, 2048), BF), V((1024, 1024), BF), V((1024, 1024), BF), V((4, 1024, 256), BF),
                        DMA((7,)), DMA((3, 3)), DMA((3, 3)), DMA((3, 3)), DMA((3, 3)), DMA((3, 7)), DMA((3, 4)),
                        DMA((8,)), DMA((8,)), DMA((8,)), DMA((8,)), DMA((8,)), DMA((8,)), DMA((16,)), DMA((16,)),
                        DMA((1,)), DMA((1,)), DMA((2,)), DMA((2,)), DMA((2,)), DMA((2,)), DMA((4,)), DMA((4,)),
                        DMA((4, 3)), DMA((4, 3)), DMA((4, 6)), DMA((2,))],
        compiler_params=pltpu.CompilerParams(collective_id=1, has_side_effects=True, vmem_limit_bytes=VLIM),
    )(x, dy, docs, qkv, ff, qb, fb, small, fc2, dense, cos, sin)


def lanes_of(shape):
    return lax.broadcasted_iota(jnp.int32, shape, len(shape) - 1)


def partner(t):
    low = lax.rem(lanes_of(t.shape), 64) < 16
    return jnp.where(low, pltpu.roll(t, 112, 1), pltpu.roll(t, 16, 1))


def dot_nt(a, b):
    return lax.dot_general(a, b, (((1,), (1,)), ((), ())), preferred_element_type=F32)


def dot_tn(a, b):
    return lax.dot_general(a, b, (((0,), (0,)), ((), ())), preferred_element_type=F32)


def attention_kernel(slot_of, a, docs, cos, sin, out, sums, seq, att, dq, dk, dv):
    def where_is(p):
        r = slot_of[p]
        ctx = lax.div(r, 2)
        return lax.rem(ctx, 4), lax.div(ctx, 4), pl.ds(pl.multiple_of(lax.rem(r, 2) * 64, 64), 64)

    for p in range(16):
        g, yy, rows = where_is(p)
        seq[64 * p : 64 * p + 64, :] = a[g, yy, 0, rows, :]
    dk[...] = jnp.zeros_like(dk)
    dv[...] = jnp.zeros_like(dv)
    scale = 0.125
    low = lanes_of((256, 128)) < 64
    for i in range(4):
        k0 = max(0, i - 2) * 256
        kn = 256 * (i + 1) - k0
        rq, rk = slice(256 * i, 256 * i + 256), slice(k0, k0 + kn)
        qk, vd = seq[rq, 0:128], seq[rq, 128:256]
        kk, vv = seq[rk, 0:128], seq[rk, 128:256]
        zero = jnp.zeros((256, 128), F32)
        qs = jnp.where(low, zero, pltpu.roll(qk.astype(F32), 64, 1)).astype(BF)
        dsf = jnp.where(low, pltpu.roll(vd.astype(F32), 64, 1), zero)
        s = dot_nt(qs, kk) * scale
        qpos = 256 * i + lax.broadcasted_iota(jnp.int32, (256, kn), 0)
        kpos = k0 + lax.broadcasted_iota(jnp.int32, (256, kn), 1)
        own = jnp.broadcast_to(docs[0, 0:1, rq].astype(F32), (128, 256)).T[:, 0:1]
        mask = (kpos <= qpos) & (docs[0, 0:1, rk].astype(F32) == own)
        s = jnp.where(mask, s, NEG)
        top = jnp.max(s, axis=-1, keepdims=True)
        e = jnp.where(mask, jnp.exp(s - top), 0.0)
        inv = 1.0 / jnp.sum(e, axis=-1, keepdims=True)
        o = jnp.dot(e.astype(BF), vv, preferred_element_type=F32) * inv
        ob = o.astype(BF)
        att[rq, :] = ob.astype(F32)
        delta = jnp.sum(dsf * ob.astype(F32), axis=-1, keepdims=True)
        pr = e * inv
        dv[rk, :] += dot_tn(pr.astype(BF), vd)
        dp = dot_nt(dsf.astype(BF), vv)
        ds = (pr * (dp - delta) * scale).astype(BF)
        dq[rq, :] = jnp.dot(ds, kk, preferred_element_type=F32)
        dk[rk, :] += dot_tn(ds, qk)
    tot = jnp.zeros((8, 256), F32)
    half = lanes_of((64, 128)) < 64
    s1 = jnp.zeros((1, 128), F32)
    s2 = jnp.zeros((1, 128), F32)
    for p in range(16):
        rows = slice(64 * p, 64 * p + 64)
        g, yy, place_rows = where_is(p)
        t = jnp.where(half, pltpu.roll(dq[rows, :], 64, 1), pltpu.roll(dk[rows, :], 64, 1))
        t = t * cos[rows, :] - partner(t) * sin[rows, :]
        u = jnp.where(half, pltpu.roll(dv[rows, :], 64, 1), pltpu.roll(att[rows, :], 64, 1))
        s1 += jnp.sum(t, axis=0, keepdims=True)
        s2 += jnp.sum(u, axis=0, keepdims=True)
        out[g, yy, 0, place_rows, 0:128] = t.astype(BF)
        out[g, yy, 0, place_rows, 128:256] = u.astype(BF)
    sums[0, :, 0:128] = jnp.broadcast_to(s1, (8, 128))
    sums[0, :, 128:256] = jnp.broadcast_to(s2, (8, 128))


def attention(slot_of, a, docs, cos, sin):
    sd = jax.ShapeDtypeStruct
    blk = pl.BlockSpec((4, 2, 1, 128, 256), lambda s, t: (0, 0, s, 0, 0))
    return pl.pallas_call(
        attention_kernel,
        name="attention",
        grid_spec=pltpu.PrefetchScalarGridSpec(
            num_scalar_prefetch=1,
            grid=(4,),
            in_specs=[
                blk,
                pl.BlockSpec((1, 8, 1024), lambda s, t: (s, 0, 0)),
                pl.BlockSpec((1024, 128), lambda s, t: (0, 0)),
                pl.BlockSpec((1024, 128), lambda s, t: (0, 0)),
            ],
            out_specs=(blk, pl.BlockSpec((1, 8, 256), lambda s, t: (s, 0, 0))),
            scratch_shapes=[pltpu.VMEM((1024, 256), BF)] + [pltpu.VMEM((1024, 128), F32)] * 4,
        ),
        out_shape=(sd((4, 2, 4, 128, 256), BF), sd((4, 8, 256), F32)),
        compiler_params=pltpu.CompilerParams(vmem_limit_bytes=VLIM),
    )(slot_of, a, docs, cos, sin)


def add_rows(dst, srcs, rows, out=None, step=16):
    out = dst if out is None else out

    def body(i, carry):
        sl = pl.ds(pl.multiple_of(i * step, step), step)
        v = dst[sl, :].astype(F32)
        for s in srcs:
            v = v + s[sl, :].astype(F32)
        out[sl, :] = v.astype(out.dtype)
        return carry

    lax.fori_loop(0, rows // step, body, 0)


def reduce_kernel(att, normed_i, dy_i, x_i, act_i, dup_i, wc_i, w2_i, sums, dsum,
                  yo, o1, o2, eo, dbo,
                  nrm, dy, wc, w2, dpr, up2, rec, ysend, yr, ud, own, r1, st1, r2, s1, st2, s2, thin2, flip, xst, mu, rs, acc, ev, t1, t2, d1,
                  hss, hsr, hl, ld, xl, yss, yrs, uss, urs, k1s, k1r, x1s, x1r, a1s, a1r,
                  k2s, k2r, x2s, x2r, eks, ekr, exs, exr, eas, ear, dbs, dbr, fl):
    n = Net()
    far = {"ctx": n.ctx + 2 * (1 - 2 * n.x) + 1 - 2 * n.c, "fsdp": n.z}
    n.barrier(more=(far,))
    z0 = lax.div(n.z, 2)
    zf = 1 - z0

    def halves(k):
        yy = n.y if k % 2 else n.yb
        tile = 0 if k >= 2 else 1
        return pl.ds(pl.multiple_of(yy * 512, 512), 512), pl.ds(128 * tile, 128)

    for k in range(4):
        rows, lanes = halves(k)
        for i, (to, gg) in enumerate(((far, 2 * n.xb + n.cb), (n.to_x, 2 * n.xb + n.c), (n.to_c, 2 * n.x + n.cb))):
            n.go(remote(att.at[gg, rows, lanes], rec.at[n.g, rows, lanes], hss.at[k, i], hsr.at[k, i], to))
    keep = pltpu.make_async_copy(att.at[n.g], rec.at[n.g], hl.at[0])
    loads = [
        pltpu.make_async_copy(dy_i, dy, ld.at[0]),
        pltpu.make_async_copy(act_i, up2.at[:, pl.ds(0, 1024)], ld.at[1]),
        pltpu.make_async_copy(w2_i, w2, ld.at[2]),
        pltpu.make_async_copy(dup_i, dpr.at[:, pl.ds(768, 1024)], ld.at[3]),
        pltpu.make_async_copy(normed_i, nrm, ld.at[4]),
        pltpu.make_async_copy(wc_i, wc, ld.at[5]),
    ]
    for copy in loads[:2] + [keep] + loads[2:]:
        copy.start()

    def heads_in(k):
        rows, lanes = halves(k)
        for i, gg in enumerate((2 * n.xb + n.cb, 2 * n.xb + n.c, 2 * n.x + n.cb)):
            arrive(rec.at[gg, rows, lanes], hsr.at[k, i])

    low = lanes_of((64, 128)) < 64

    def split(k):
        yy = n.y if k % 2 else n.yb

        def body(i, carry):
            sl = pl.ds(pl.multiple_of(yy * 512 + 64 * i, 64), 64)
            for p in range(2):
                a, b = rec[2 * p, sl, 128:256].astype(F32), rec[2 * p + 1, sl, 128:256].astype(F32)
                up2[sl, 1024 + 128 * p : 1152 + 128 * p] = jnp.where(low, pltpu.roll(a, 64, 1), b).astype(BF)
                dpr[sl, 512 + 128 * p : 640 + 128 * p] = jnp.where(low, a, pltpu.roll(b, 64, 1)).astype(BF)
            return carry

        lax.fori_loop(0, 8, body, 0)

    def pair_rows(yy, zp):
        return pl.ds(pl.multiple_of((yy * 4 + 2 * zp) * 128, 256), 256)

    def into(dst, zp, cols, value):
        dst(2 * zp)[:, cols] = value[0:128].astype(BF)
        dst(2 * zp + 1)[:, cols] = value[128:256].astype(BF)

    def chunks(count, width, body):
        def step(i, carry):
            body(pl.ds(pl.multiple_of(i * width, width), width))
            return carry

        lax.fori_loop(0, count, step, 0)

    def y_pair(yy, zp, dst):
        rows = pair_rows(yy, zp)

        def body(cols):
            into(dst, zp, cols, jnp.dot(up2[rows, :], w2[:, cols], preferred_element_type=F32))

        chunks(4, 512, body)

    def dn_pair(yy, zp, dst):
        rows = pair_rows(yy, zp)
        load = pltpu.make_async_copy(x_i.at[rows], xst, xl.at[0])
        load.start()
        load.wait()

        def stats(i, carry):
            sl = pl.ds(pl.multiple_of(32 * i, 32), 32)
            xf = xst[sl, :].astype(F32)
            mean = jnp.mean(xf, axis=-1, keepdims=True)
            cen = xf - mean
            mu[sl, :] = jnp.broadcast_to(mean, (32, 128))
            rs[sl, :] = jnp.broadcast_to(lax.rsqrt(jnp.mean(cen * cen, axis=-1, keepdims=True) + EPS), (32, 128))
            return carry

        lax.fori_loop(0, 8, stats, 0)

        def body(cols):
            d = dot_nt(dpr[rows, :], wc[cols, :])
            xh = (xst[:, cols].astype(F32) - mu[:, 0:1]) * rs[:, 0:1]
            acc[0:1, cols] += jnp.sum(d * xh, axis=0, keepdims=True)
            acc[1:2, cols] += jnp.sum(d, axis=0, keepdims=True)
            into(dst, zp, cols, d)

        chunks(8, 256, body)

    def send_y(t, buf, k, j):
        n.go(remote(buf, yr.at[k, t], yss.at[t, j], yrs.at[t, k], n.to_y))

    def w1_rows(yy, xx, cc):
        return pl.ds(pl.multiple_of((yy * 16 + xx * 8 + cc * 4) * 64, 256), 256)

    def w1_part(yy, xx, cc, write):
        flip[...] = nrm[:, w1_rows(yy, xx, cc)].T
        chunks(7, 256, lambda cols: write(cols, jnp.dot(flip[...], dpr[:, cols], preferred_element_type=F32)))

    def w2_part(gg, write):
        flip[...] = up2[:, pl.ds(pl.multiple_of(gg * 256, 256), 256)].T
        chunks(4, 512, lambda cols: write(cols, jnp.dot(flip[...], dy[:, cols], preferred_element_type=F32)))

    wide, thin = pl.ds(0, 256), pl.ds(256, 64)
    acc[...] = jnp.zeros_like(acc)

    loads[0].wait()
    loads[1].wait()

    def other_wide(xx, carry):
        def write(cols, value):
            st2[xx, 0:256, cols] = value.astype(BF)

        w2_part(2 * xx + n.cb, write)
        return carry

    lax.fori_loop(0, 2, other_wide, 0)
    for xx in range(2):
        n.go(remote(st2.at[xx, wide], s1.at[xx, wide], k2s.at[xx, 0], k2r.at[xx, 0], n.to_c))
    loads[2].wait()
    keep.wait()
    heads_in(0)
    split(0)
    zn = n.z + 1 - 2 * lax.rem(n.z, 2)
    y_pair(n.yb, zf, lambda k: ysend.at[k])
    send_y(0, ysend.at[3 * zf], 3 * zf, 0)
    send_y(0, ysend.at[1 + zf], 1 + zf, 1)
    y_pair(n.yb, z0, lambda k: ysend.at[k])
    send_y(0, ysend.at[zn], zn, 2)
    send_y(0, ysend.at[n.z], n.z, 3)
    heads_in(1)
    split(1)

    def own_y(i, carry):
        y_pair(n.y, i, lambda k: own.at[k, 0])
        return carry

    lax.fori_loop(0, 2, own_y, 0)
    flip[...] = up2[:, 1024:1280].T

    def thin_part(cols):
        four = jnp.dot(flip[...], dy[:, cols], preferred_element_type=F32)
        for xx in range(2):
            a, b = four[128 * xx : 128 * xx + 64], four[128 * xx + 64 : 128 * xx + 128]
            st2[xx, 256:320, cols] = jnp.where(n.c == 0, b, a).astype(BF)
            thin2[64 * xx : 64 * xx + 64, cols] = jnp.where(n.c == 0, a, b).astype(BF)

    chunks(4, 512, thin_part)
    for xx in range(2):
        n.go(remote(st2.at[xx, thin], s1.at[xx, thin], k2s.at[xx, 1], k2r.at[xx, 1], n.to_c))

    def w2_own(xx):
        arrive(s1.at[xx, wide], k2r.at[xx, 0])

        def write(cols, value):
            s1[xx, 0:256, cols] = (s1[xx, 0:256, cols].astype(F32) + value).astype(BF)

        w2_part(2 * xx + n.c, write)
        arrive(s1.at[xx, thin], k2r.at[xx, 1])
        mine = pl.ds(pl.multiple_of(64 * xx, 64), 64)
        s1[xx, 256:320, :] = (s1[xx, 256:320, :].astype(F32) + thin2[mine, :].astype(F32)).astype(BF)

    w2_own(n.xb)
    w2_own(n.x)
    outer = (n.z == 0) | (n.z == 3)
    inner = (n.z == 1) | (n.z == 2)

    def forward(t, j, who):
        k = (3 * zf, 1 + zf, zn)[j]
        up = jnp.where(k > n.z, 1, 0)
        slot = k + up
        block = own.at[k, t]

        @pl.when(who)
        def _():
            arrive(yr.at[k, t], yrs.at[t, k])
            if who is inner:
                arrive(ud.at[slot, t], urs.at[t, slot])
                add_rows(block, [yr.at[k, t], ud.at[slot, t]], 128)
            else:
                add_rows(block, [yr.at[k, t]], 128)

        to = {"ctx": n.ctx, "fsdp": n.z + 2 * up - 1}
        n.go(remote(block, ud.at[slot, t], uss.at[t, j], urs.at[t, slot], to), who)

    forward(0, 0, outer)
    heads_in(2)
    heads_in(3)

    def whole(i, carry):
        sl = pl.ds(pl.multiple_of(64 * i, 64), 64)
        for g in range(4):
            dpr[sl, 128 * g : 128 * g + 128] = rec[g, sl, 0:128]
        return carry

    lax.fori_loop(0, 16, whole, 0)
    loads[3].wait()
    loads[4].wait()

    def staged(k):
        xx = n.xb + (k // 2) * (1 - 2 * n.xb) if isinstance(k, int) else n.xb + lax.div(k, 2) * (1 - 2 * n.xb)
        yy = n.yb + (k % 2) * (1 - 2 * n.yb) if isinstance(k, int) else n.yb + lax.rem(k, 2) * (1 - 2 * n.yb)
        slot = k % 2 if isinstance(k, int) else lax.rem(k, 2)
        return yy, xx, remote(st1.at[slot], r1.at[yy * 2 + xx], k1s.at[k], k1r.at[yy * 2 + xx], n.to_c), slot

    def other_rows(k, carry):
        yy, xx, copy, slot = staged(k)

        @pl.when(k >= 2)
        def _():
            staged(k - 2)[2].wait_send()

        def write(cols, value):
            st1[slot, :, cols] = value.astype(BF)

        w1_part(yy, xx, n.cb, write)
        copy.start()
        return carry

    lax.fori_loop(0, 2, other_rows, 0)

    def w1_own(yy, xx):
        block = r1.at[yy * 2 + xx]
        arrive(block, k1r.at[yy * 2 + xx])

        def write(cols, value):
            block[:, cols] = (block[:, cols].astype(F32) + value).astype(BF)

        w1_part(yy, xx, n.c, write)

    def finish(t):
        k = n.z
        arrive(yr.at[k, t], yrs.at[t, k])

        @pl.when(n.z > 0)
        def _():
            arrive(ud.at[k + 1, t], urs.at[t, k + 1])

        @pl.when(n.z < 3)
        def _():
            arrive(ud.at[k, t], urs.at[t, k])

        @pl.when(n.z == 0)
        def _():
            add_rows(own.at[k, t], [yr.at[k, t], ud.at[k, t]], 128, yo.at[t])

        @pl.when(n.z == 3)
        def _():
            add_rows(own.at[k, t], [yr.at[k, t], ud.at[k + 1, t]], 128, yo.at[t])

        @pl.when(inner)
        def _():
            add_rows(own.at[k, t], [yr.at[k, t], ud.at[k, t], ud.at[k + 1, t]], 128, yo.at[t])

    for yy in (n.yb, n.y):
        w1_own(yy, n.xb)
        n.go(remote(r1.at[yy * 2 + n.xb], r2.at[yy], x1s.at[yy], x1r.at[yy], n.to_x))
    lax.fori_loop(2, 4, other_rows, 0)
    forward(0, 1, outer)
    n.go(remote(s1.at[n.xb], s2, x2s.at[0], x2r.at[0], n.to_x))
    loads[5].wait()

    def spare_at(k):
        return w2.at[pl.ds(pl.multiple_of(128 * k, 128), 128)]

    dn_pair(n.yb, zf, spare_at)
    send_y(1, spare_at(3 * zf), 3 * zf, 0)
    send_y(1, spare_at(1 + zf), 1 + zf, 1)
    forward(0, 0, inner)
    dn_pair(n.yb, z0, spare_at)
    send_y(1, spare_at(zn), zn, 2)
    send_y(1, spare_at(n.z), n.z, 3)
    forward(0, 2, outer)
    forward(0, 1, inner)
    for yy in (n.yb, n.y):
        w1_own(yy, n.x)
    def give(yy, qs):
        arrive(r2.at[yy], x1r.at[yy])
        add_rows(r1.at[yy * 2 + n.x], [r2.at[yy]], 256)
        for q in qs:
            to, _, zz = n.member(q)
            n.go(remote(r1.at[yy * 2 + n.x, pl.ds(pl.multiple_of(zz * 64, 64), 64)], o1.at[n.m], a1s.at[q], a1r.at[q], to))

    give(n.yb, (6, 5, 7, 4))

    def own_dn(i, carry):
        dn_pair(n.y, i, lambda k: own.at[k, 1])
        return carry

    lax.fori_loop(0, 2, own_dn, 0)
    forward(0, 2, inner)
    ones = jnp.ones((8, 1024), BF)
    d1[0] = jnp.dot(ones, dy[...], preferred_element_type=F32)
    tot = sums[0, 0:1, :] + sums[1, 0:1, :] + sums[2, 0:1, :] + sums[3, 0:1, :]
    lo1 = lanes_of((1, 128)) < 64
    zero = jnp.zeros((1, 128), F32)
    vsum = jnp.where(n.c == 0, jnp.where(lo1, tot[:, 128:256], zero), jnp.where(lo1, zero, pltpu.roll(tot[:, 128:256], 64, 1)))
    for g in range(4):
        for mm in range(8):
            e = ev.at[g * 8 + mm]
            for k in range(4):
                e[k : k + 1, :] = jnp.where(n.g == k, tot[:, 0:128], zero)
            for k in range(2):
                e[4 + k : 5 + k, :] = jnp.where(n.x == k, vsum, zero)
            for k in range(8):
                e[6 + k : 7 + k, :] = dsum[0:1, 128 * k : 128 * k + 128]
            tile = 128 * ((mm // 4) * 8 + g * 2 + (mm % 4) // 2)
            e[14:15, :] = acc[0:1, tile : tile + 128]
            e[15:16, :] = acc[1:2, tile : tile + 128]
    for xx in range(2):
        n.go(remote(ev.at[pl.ds((2 * xx + n.cb) * 8, 8)], t1.at[xx], eks.at[xx], ekr.at[xx], n.to_c))
    n.go(remote(d1.at[0], d1.at[1], dbs.at[0], dbr.at[0], n.to_c))
    forward(1, 0, outer)
    for xx in range(2):
        arrive(t1.at[xx], ekr.at[xx])
        sl = pl.ds((2 * xx + n.c) * 8, 8)
        ev[sl] = ev[sl] + t1[xx]
    arrive(d1.at[1], dbr.at[0])
    d1[2] = d1[0] + d1[1]
    n.go(remote(ev.at[pl.ds((2 * n.xb + n.c) * 8, 8)], t2, exs.at[0], exr.at[0], n.to_x))
    n.go(remote(d1.at[2], d1.at[3], dbs.at[1], dbr.at[1], n.to_x))

    forward(1, 1, outer)
    forward(1, 0, inner)
    forward(1, 2, outer)
    forward(1, 1, inner)
    give(n.y, (2, 1, 3))
    mine = pltpu.make_async_copy(r1.at[n.y * 2 + n.x, pl.ds(pl.multiple_of(n.z * 64, 64), 64)], o1.at[n.m], fl.at[0])
    mine.start()
    arrive(t2, exr.at[0])
    final = pl.ds(n.g * 8, 8)
    ev[final] = ev[final] + t2[...]
    for q in range(1, 8):
        to, yy, zz = n.member(q)
        n.go(remote(ev.at[n.g * 8 + yy * 4 + zz], eo.at[n.m], eas.at[q], ear.at[q], to))
    eo[n.m] = ev[n.g * 8 + n.m]
    arrive(d1.at[3], dbr.at[1])
    dbo[...] = d1[2] + d1[3]
    forward(1, 2, inner)
    finish(0)
    arrive(s2, x2r.at[0])
    add_rows(s1.at[n.x], [s2], 320)
    out2 = pltpu.make_async_copy(s1.at[n.x], o2, fl.at[1])
    out2.start()
    finish(1)
    for q in range(1, 8):
        yy, zz = n.source(q)
        arrive(eo.at[yy * 4 + zz], ear.at[q])
        arrive(o1.at[yy * 4 + zz], a1r.at[q])
    mine.wait()
    out2.wait()
    for k in (2, 3):
        staged(k)[2].wait_send()
    n.drain()


def reduce_all(att, normed, dy, x, act, dup, wc, w2, sums, dsum):
    sd = jax.ShapeDtypeStruct
    V = pltpu.VMEM
    return pl.pallas_call(
        reduce_kernel,
        name="reduce_all",
        out_shape=(sd((2, 128, 2048), F32), sd((8, 64, 1792), BF), sd((320, 2048), BF), sd((8, 16, 128), F32),
                   sd((8, 2048), F32)),
        in_specs=[HBM] * 8 + [VM] * 2,
        out_specs=(VM, HBM, HBM, VM, VM),
        scratch_shapes=[
            V((1024, 2048), BF), V((1024, 2048), BF), V((2048, 1792), BF), V((1280, 2048), BF),
            V((1024, 1792), BF), V((1024, 1280), BF), V((4, 1024, 256), BF),
            V((4, 128, 2048), BF), V((4, 2, 128, 2048), BF), V((5, 2, 128, 2048), BF), V((4, 2, 128, 2048), BF),
            V((4, 256, 1792), BF), V((2, 256, 1792), BF), V((2, 256, 1792), BF),
            V((2, 320, 2048), BF), V((2, 320, 2048), BF), V((320, 2048), BF), V((128, 2048), BF), V((256, 1024), BF),
            V((256, 2048), BF), V((256, 128), F32), V((256, 128), F32), V((8, 2048), F32),
            V((32, 16, 128), F32), V((2, 8, 16, 128), F32), V((8, 16, 128), F32), V((4, 8, 2048), F32),
            DMA((4, 3)), DMA((4, 3)), DMA((1,)), DMA((6,)), DMA((1,)),
            DMA((2, 4)), DMA((2, 4)), DMA((2, 3)), DMA((2, 5)),
            DMA((4,)), DMA((4,)), DMA((2,)), DMA((2,)), DMA((8,)), DMA((8,)),
            DMA((2, 2)), DMA((2, 2)), DMA((1,)), DMA((1,)),
            DMA((2,)), DMA((2,)), DMA((1,)), DMA((1,)), DMA((8,)), DMA((8,)), DMA((2,)), DMA((2,)), DMA((2,)),
        ],
        compiler_params=pltpu.CompilerParams(collective_id=3, has_side_effects=True, vmem_limit_bytes=67000000),
    )(att, normed, dy, x, act, dup, wc, w2, sums, dsum)


def finish_kernel(x, dy, yo, o1, o2, cst, y, dx, dqkv, dff, dfc2, ddense):
    low = lanes_of((64, 128)) < 64
    for i in range(16):
        yy, g, zp = i // 8, (i // 2) % 4, i % 2
        a, b = yy * 4 + 2 * zp, yy * 4 + 2 * zp + 1
        cols = slice(128 * i, 128 * i + 128)
        src = slice(128 * g, 128 * g + 128)
        even, odd = o1[a, :, src].astype(F32), o1[b, :, src].astype(F32)
        dqkv[:, cols] = jnp.where(low, even, pltpu.roll(odd, 64, 1))
        dqkv[:, 2048 + 128 * i : 2176 + 128 * i] = jnp.where(low, pltpu.roll(even, 64, 1), odd)
        src = slice(512 + 128 * (g // 2), 640 + 128 * (g // 2))
        even, odd = o1[a, :, src].astype(F32), o1[b, :, src].astype(F32)
        if g % 2 == 0:
            v = jnp.where(low, even, pltpu.roll(odd, 64, 1))
        else:
            v = jnp.where(low, pltpu.roll(even, 64, 1), odd)
        dqkv[:, 4096 + 128 * i : 4224 + 128 * i] = v
    for h in range(32):
        mm, g = (h // 16) * 4 + h % 4, (h // 4) % 4
        dff[:, 256 * h : 256 * h + 256] = o1[mm, :, 768 + 256 * g : 1024 + 256 * g].astype(F32)
    dfc2[...] = o2[0:256, :].astype(F32)
    ddense[...] = o2[256:320, :].astype(F32)

    def body(i, carry):
        sl = pl.ds(pl.multiple_of(16 * i, 16), 16)
        xf = x[sl, :].astype(F32)
        cen = xf - jnp.mean(xf, axis=-1, keepdims=True)
        rstd = lax.rsqrt(jnp.mean(cen * cen, axis=-1, keepdims=True) + EPS)
        xhat = cen * rstd
        y[sl, :] = (xf + yo[0, sl, :] + cst[2:3, :]).astype(BF)
        gr = yo[1, sl, :] * cst[0:1, :]
        dx[sl, :] = dy[sl, :].astype(F32) + rstd * (
            gr - jnp.mean(gr, axis=-1, keepdims=True) - xhat * jnp.mean(gr * xhat, axis=-1, keepdims=True)
        )
        return carry

    lax.fori_loop(0, 8, body, 0)


def finish_all(x, dy, yo, o1, o2, cst):
    sd = jax.ShapeDtypeStruct
    return pl.pallas_call(
        finish_kernel,
        name="finish_all",
        out_shape=(sd((128, 2048), BF), sd((128, 2048), F32), sd((64, 6144), F32), sd((64, 8192), F32),
                   sd((256, 2048), F32), sd((64, 2048), F32)),
        in_specs=[VM] * 6,
        out_specs=(VM,) * 6,
        compiler_params=pltpu.CompilerParams(vmem_limit_bytes=VLIM),
    )(x, dy, yo, o1, o2, cst)


def stored_columns(a):
    rows = a.shape[1]
    qk = a[:, :, :512].reshape(2, 4, rows, 4, 2, 64).transpose(2, 4, 0, 3, 1, 5).reshape(rows, 2, 2048)
    v = a[:, :, 512:768].reshape(2, 4, rows, 4, 64).transpose(2, 0, 3, 1, 4).reshape(rows, 1, 2048)
    f = a[:, :, 768:1792].reshape(2, 4, rows, 4, 256).transpose(2, 0, 3, 1, 4).reshape(rows, 8192)
    return jnp.concatenate([qk, v], axis=1).reshape(rows, 6144), f


def rotary_lanes(pos):
    lane = jnp.arange(128, dtype=jnp.int32) % 64
    freqs = jnp.exp(-(2.0 * (lane % (ROT // 2)).astype(F32) / ROT) * math.log(10000.0))
    angles = pos.astype(F32)[:, None] * freqs[None]
    turns = lane < ROT
    sign = jnp.where(turns, jnp.where(lane < ROT // 2, -1.0, 1.0), 0.0)
    return jnp.where(turns, jnp.cos(angles), 1.0), jnp.sin(angles) * sign


def fast_device(
    block_input, output_grad, segment, slots, ln_gain, ln_bias, qkv_w, qkv_b, dense_w, dense_b, fc1_w, fc1_b, fc2_w, fc2_b
):
    ctx, y, x, c, z = place()
    g, m = x * 2 + c, y * 4 + z
    index = ctx * 4 + z
    xb, dyb = block_input[0], output_grad[0]

    def spread(piece, total):
        count = piece.shape[0]
        own = jnp.arange(total, dtype=jnp.int32) // count == index
        return jnp.where(own, jnp.tile(piece, total // count), jnp.zeros((), BF))

    docs = jnp.broadcast_to(segment.astype(BF), (8, 1024))
    qb = jnp.broadcast_to(spread(qkv_b, 6144)[None], (8, 6144))
    fb = jnp.broadcast_to(spread(fc1_b, 8192)[None], (8, 8192))
    vecs = jnp.stack([spread(v, 2048) for v in (ln_gain, ln_bias, dense_b, fc2_b)])
    rest = jnp.pad(vecs[:, 1792:].reshape(1, 1024), ((0, 0), (0, 768)))
    small = jnp.concatenate([jnp.zeros((1, 1792), BF), vecs[:, :1792], rest, jnp.zeros((2, 1792), BF)], axis=0)
    pairs = lax.dynamic_slice_in_dim(slots.reshape(2, 4, 2), g, 1, 1).reshape(4)
    rows = (pairs[:, None] * 64 + jnp.arange(64, dtype=jnp.int32)[None]).reshape(256)
    cos2, sin2 = rotary_lanes(rows)
    cos, sin = rotary_lanes(jnp.arange(1024, dtype=jnp.int32))
    xg, dg, docg, normed, act, dup, wc, w2g, heads, dsum, cst = gather_all(
        xb, dyb, docs, qkv_w, fc1_w, qb, fb, small, fc2_w, dense_w, cos2, sin2
    )
    slot_of = jnp.sum(jnp.where(slots[None, :] == jnp.arange(16, dtype=jnp.int32)[:, None], jnp.arange(16, dtype=jnp.int32)[None, :], 0), axis=1)
    att, sums = attention(slot_of, heads.reshape(4, 2, 4, 128, 256), docg, cos, sin)
    yo, o1, o2, eo, dbo = reduce_all(att.reshape(4, 1024, 256), normed, dg, xg, act, dup, wc, w2g, sums, dsum)
    out, dx, g_qkv_w, g_fc1_w, g_fc2_w, g_dense_w = finish_all(xb, dyb, yo, o1, o2, cst)
    eo = eo.reshape(8, 2048)
    sq, sf = stored_columns(eo[:, None, :1792])
    g_qkv_b = lax.dynamic_slice_in_dim(sq[0], index * 192, 192, 0)
    g_fc1_b = lax.dynamic_slice_in_dim(sf[0], index * 256, 256, 0)
    tiles = jnp.sum(eo[:, 1792:].reshape(8, 2, 2, 64), axis=0)
    both = lax.dynamic_slice_in_dim(tiles, z % 2, 1, 1)
    g_db = lax.dynamic_slice_in_dim(dbo[0], index * 64, 64, 0)
    return (out[None], dx[None], both[0, 0], both[1, 0], g_qkv_w, g_qkv_b, g_dense_w, g_db, g_fc1_w, g_fc1_b, g_fc2_w, g_db)


def solution(mesh):
    in_specs = (
        P("fsdp", "ctx", None),
        P("fsdp", "ctx", None),
        P("fsdp", None),
        P(),
        P(("ctx", "fsdp")),
        P(("ctx", "fsdp")),
        P(("ctx", "fsdp"), None),
        P(("ctx", "fsdp")),
        P(("ctx", "fsdp"), None),
        P(("ctx", "fsdp")),
        P(("ctx", "fsdp"), None),
        P(("ctx", "fsdp")),
        P(("ctx", "fsdp"), None),
        P(("ctx", "fsdp")),
    )
    out_specs = (
        P("fsdp", "ctx", None),
        P("fsdp", "ctx", None),
        P(("ctx", "fsdp")),
        P(("ctx", "fsdp")),
        P(("ctx", "fsdp"), None),
        P(("ctx", "fsdp")),
        P(("ctx", "fsdp"), None),
        P(("ctx", "fsdp")),
        P(("ctx", "fsdp"), None),
        P(("ctx", "fsdp")),
        P(("ctx", "fsdp"), None),
        P(("ctx", "fsdp")),
    )
    small = mesh.shape["ctx"] == 8 and mesh.shape["fsdp"] == 4
    return jax.shard_map(
        fast_device if small else per_device, mesh=mesh, in_specs=in_specs, out_specs=out_specs, check_vma=False
    )
```

profile of v0, /device:TPU:8, one launch (start us, length us, event | category | flops | bytes accessed | tf_op | source)
XLA Modules:
  0.0 337.0 jit_solution(4591904822272152146)
XLA Ops:
  0.7 0.7 reshape.242
  1.7 1.2 fusion.3
  3.0 0.7 tile.62
  3.7 0.7 tile.64
  4.5 0.7 tile.28
  5.2 0.7 tile.60
  6.2 0.7 fusion.12.small
  6.9 0.7 broadcast_in_dim.109.fb
  7.6 0.7 tile.24
  8.4 0.7 broadcast_in_dim.107.qb
  9.1 0.7 convert_reduce_fusion
  9.8 0.6 broadcast_in_dim.105.docs
  10.4 134.4 %gather_all.1 = (bf16[1024,2048]{1,0:T(8,128)(2,1)}, bf16[1024,2048]{1,0:T(8,128)(2,1)}, bf16[8,8,1024]{2,1,0:T(8,128)(2,1)}, bf16[1024,2048]{1,0:T(8,128)(2,1)}...) custom-call(bf16[128,2048]{1,0:T(8,128)(2,1)} %bitcast.38, ...), custom_call_target="tpu_custom_call" | custom-call | tf_op jit(solution)/shard_map/gather_all/pallas_call | solution.py:659
  144.8 3.1 fusion.1
  147.9 0.6 select_reduce_fusion.slot_of
  148.5 24.3 %attention.1 = (bf16[4,2,4,128,256]{4,3,2,1,0:T(8,128)(2,1)}, f32[4,8,256]{2,1,0:T(8,128)}) custom-call(s32[16]{0:T(128)} %select_reduce_fusion.slot_of, bf16[4,2,4,128,256]{4,3,2,1,0:T(8,128)(2,1)} %bitcast.37, bf16[8,8,1024]{2,1,0:T(8,128)(2,1)} %get-tuple-element.37.docs, f32[1024,128]{1,0:T(8,128)} %get-tuple-element.61.cos, ...), custom_call_target="tpu_custom_call" | custom-call | tf_op jit(solution)/shard_map/attention/pallas_call | solution.py:757
  172.8 150.6 %reduce_all.1 = (f32[2,128,2048]{2,1,0:T(8,128)}, bf16[8,64,1792]{2,1,0:T(8,128)(2,1)}, bf16[320,2048]{1,0:T(8,128)(2,1)}, f32[8,16,128]{2,1,0:T(8,128)}, f32[8,2048]{1,0:T(8,128)}) custom-call(bf16[4,1024,256]{2,1,0:T(8,128)(2,1)} %bitcast.42, bf16[1024,2048]{1,0:T(8,128)(2,1)} %get-tuple-element.39.normed_i, bf16[1024,2048]{1,0:T(8,128)(2,1)} %get-tuple-element.40.dy_i, ...), custom_call_target="tpu_custom_call" | custom-call | tf_op jit(solution)/shard_map/reduce_all/pallas_call | solution.py:1161
  323.5 0.9 copy.37
  324.8 0.6 dynamic_slice.19
  325.4 8.8 %finish_all.1 = (bf16[128,2048]{1,0:T(8,128)(2,1)}, f32[128,2048]{1,0:T(8,128)}, f32[64,6144]{1,0:T(8,128)}, f32[64,8192]{1,0:T(8,128)}, f32[256,2048]{1,0:T(8,128)}, /*index=5*/f32[64,2048]{1,0:T(8,128)}) custom-call(bf16[128,2048]{1,0:T(8,128)(2,1)} %bitcast.39, bf16[128,2048]{1,0:T(8,128)(2,1)} %bitcast.41, f32[2,128,2048]{2,1,0:T(8,128)} %get-tuple-element.48.yo, ...), custom_call_target="tpu_custom_call" | custom-call | tf_op jit(solution)/shard_map/finish_all/pallas_call | solution.py:1227
  334.4 0.5 fusion.19
  335.0 0.6 dynamic_slice.22
  335.6 0.8 slice.38
  336.5 0.5 copy.39
  (49 shorter events, 1.7 us)
Async XLA Ops:
  0.6 6.3 %copy-start = (bf16[256]{0:T(256)(128)(2,1)S(1)}, bf16[256]{0:T(256)(128)(2,1)}, u32[]{:S(2)}) copy-start(bf16[256]{0:T(256)(128)(2,1)} %param.25) | copy-start | bytes 1540
  10.4 137.5 %copy-start.1 = (s32[16]{0:T(128)S(1)}, s32[16]{0:T(128)}, u32[]{:S(2)}) copy-start(s32[16]{0:T(128)} %param.17) | copy-start | bytes 196
  336.5 0.5 copy-start.2
where the time goes:
time: 340 us; the launch traced here: 337 us
  Pallas kernels  318 us (94%)
  local copies, waits for them, and re-layouts  11.4 us (3%)
  other arithmetic  6.65 us (2%)
    pallas_call x1, Pallas kernels, reduce_all(): pl.pallas_call(reduce_kernel, name='reduce_all', out_shape=(sd((2, 128, 2...  151 us
    pallas_call x1, Pallas kernels, gather_all(): pl.pallas_call(gather_kernel, name='gather_all', out_shape=(sd((1024, 204...  134 us
    pallas_call x1, Pallas kernels, attention(): pl.pallas_call(attention_kernel, name='attention', grid_spec=pltpu.Prefet...  24.3 us
    pallas_call x1, Pallas kernels, finish_all(): pl.pallas_call(finish_kernel, name='finish_all', out_shape=(sd((128, 2048...  8.82 us

commit v1 on v0

--- a/solution.py
+++ b/solution.py
@@ -410,19 +410,21 @@
         for g in range(4):
             h = first + 4 * g
             dst(mm, 128 * g, join(tile(0, h), tile(2048, h), odd))
-            dst(mm, 768 + 256 * g, ff[:, 256 * h : 256 * h + 256])
+            if ff is not None:
+                dst(mm, 768 + 256 * g, ff[:, 256 * h : 256 * h + 256])
         for k in range(2):
             h = first + 8 * k
             dst(mm, 512 + 128 * k, join(tile(4096, h), tile(4096, h + 4), odd))
 
 
-def gather_kernel(x, dy, docs, qkv, ff, qb, fb, small, fc2, dense, cos, sin,
-                  xg, dg, docg, normed_o, act_o, dup_o, wc_o, w2_o, heads, dsum, cst,
-                  xv, dv, wc, w2g, eg, ws, es, nrm, act, dup, hs,
+def gather_kernel(slots, x, dy, seg, qkv, ff, pack, fc2, dense,
+                  xg, dg, docg, normed_o, act_o, dup_o, wc_o, w2_o, heads, dsum, cst, cosp, sinp,
+                  docs, qb, cos, sin, xv, dv, wc, w2g, eg, ws, es, nrm, act, dup, hs,
                   loc, us, ur, ds_, dr, ys, yr, as_, ar, es_, er,
                   wxs, wxr, wks, wkr, exs, exr, eks, ekr, fxs, fxr, fks, fkr, hss, hsr, hl, wb):
     n = Net()
     far = {"ctx": n.ctx + 2 * (1 - 2 * n.x) + 1 - 2 * n.c, "fsdp": n.z}
+    docs[...] = jnp.broadcast_to(seg[...].astype(F32), (8, 1024)).astype(BF)
     n.barrier(more=(far,))
 
     def wrow(yy, xx, cc, zz):
@@ -457,13 +459,37 @@
     def put_w(mm, col, value):
         ws[mm, :, col : col + value.shape[1]] = value
 
+    low8 = lanes_of((8, 128)) < 64
+    zero8 = jnp.zeros((8, 128), F32)
+    index = n.ctx * 4 + n.z
+    tile, odd = lax.div(index, 2), lax.rem(index, 2)
+    qb[...] = jnp.zeros_like(qb)
+    b0 = jnp.broadcast_to(pack[4:5, 0:128].astype(F32), (8, 128))
+    b1 = jnp.broadcast_to(pack[4:5, 128:256].astype(F32), (8, 128))
+    r0, r1 = pltpu.roll(b0, 64, 1), pltpu.roll(b1, 64, 1)
+    first = pl.multiple_of((tile * 3 + odd) * 128, 128)
+    qb[:, pl.ds(first, 128)] = jnp.where(odd == 0, b0, jnp.where(low8, zero8, r0)).astype(BF)
+    qb[:, pl.ds(pl.multiple_of(first + 128, 128), 128)] = jnp.where(odd == 0, b1, jnp.where(low8, r0, r1)).astype(BF)
+    es[...] = jnp.zeros_like(es)
+
     def put_e(mm, col, value):
         es[mm, 0:1, col : col + value.shape[1]] = value[0:1]
 
-    for mm in range(8):
-        es[mm] = small[...]
     head_tiles((qkv, ff), put_w, 64)
-    head_tiles((qb, fb), put_e, 8)
+    head_tiles((qb, None), put_e, 8)
+    es[n.m, 0:1, pl.ds(pl.multiple_of(768 + 256 * n.g, 256), 256)] = pack[5:6, :]
+    for r in range(4):
+        v = pack[r : r + 1, 0:128].astype(F32)
+        own64 = jnp.where(odd == 0, v, pltpu.roll(v, 64, 1)).astype(BF)
+        for mm in range(8):
+            @pl.when(tile < 14)
+            def _():
+                es[mm, r + 1 : r + 2, pl.ds(pl.multiple_of(128 * tile, 128), 128)] = own64
+
+            @pl.when(tile >= 14)
+            def _():
+                es[mm, 5:6, pl.ds(pl.multiple_of(256 * r + 128 * (tile - 14), 128), 128)] = own64
+
     for q in (4, 1, 3, 5, 7, 2, 6):
         to, yy, zz = n.member(q)
         n.go(remote(es.at[yy * 4 + zz], eg.at[n.g * 8 + n.m], es_.at[q], er.at[q], to))
@@ -484,6 +510,27 @@
     ]
     for copy in local:
         copy.start()
+
+    lane = lax.rem(lanes_of((64, 128)), 64)
+    freqs = jnp.exp(-(2.0 * lax.rem(lane, ROT // 2).astype(F32) / ROT) * math.log(10000.0))
+    turns = lane < ROT
+    sign = jnp.where(turns, jnp.where(lane < ROT // 2, -1.0, 1.0), 0.0)
+    row64 = lax.broadcasted_iota(jnp.int32, (64, 128), 0)
+
+    def turn(start):
+        angles = (start + row64).astype(F32) * freqs
+        return jnp.where(turns, jnp.cos(angles), 1.0), jnp.sin(angles) * sign
+
+    for k in range(4):
+        rows64 = slice(64 * k, 64 * k + 64)
+        cos[rows64, :], sin[rows64, :] = turn(slots[(k // 2) * 8 + 2 * n.g + k % 2] * 64)
+
+    def table_rows(i, carry):
+        sl = pl.ds(pl.multiple_of(64 * i, 64), 64)
+        cosp[sl, :], sinp[sl, :] = turn(64 * i)
+        return carry
+
+    lax.fori_loop(0, 16, table_rows, 0)
 
     def line(d, ps):
         below, above = n.z >= d, n.z + d <= 3
@@ -653,7 +700,7 @@
     n.drain()
 
 
-def gather_all(x, dy, docs, qkv, ff, qb, fb, small, fc2, dense, cos, sin):
+def gather_all(slots, x, dy, seg, qkv, ff, pack, fc2, dense):
     sd = jax.ShapeDtypeStruct
     V = pltpu.VMEM
     return pl.pallas_call(
@@ -661,10 +708,11 @@
         name="gather_all",
         out_shape=(sd((1024, 2048), BF), sd((1024, 2048), BF), sd((8, 8, 1024), BF), sd((1024, 2048), BF),
                    sd((1024, 1024), BF), sd((1024, 1024), BF), sd((2048, 1792), BF), sd((1280, 2048), BF),
-                   sd((4, 1024, 256), BF), sd((8, 1024), F32), sd((8, 2048), F32)),
-        in_specs=[VM] * 12,
-        out_specs=(HBM, HBM, VM, HBM, HBM, HBM, HBM, HBM, HBM, VM, VM),
-        scratch_shapes=[V((1024, 2048), BF), V((1024, 2048), BF), V((2048, 1792), BF), V((1280, 2048), BF),
+                   sd((4, 1024, 256), BF), sd((8, 1024), F32), sd((8, 2048), F32), sd((1024, 128), F32), sd((1024, 128), F32)),
+        in_specs=[pl.BlockSpec(memory_space=pltpu.SMEM)] + [VM] * 8,
+        out_specs=(HBM, HBM, VM, HBM, HBM, HBM, HBM, HBM, HBM, VM, VM, VM, VM),
+        scratch_shapes=[V((8, 1024), BF), V((8, 6144), BF), V((256, 128), F32), V((256, 128), F32),
+                        V((1024, 2048), BF), V((1024, 2048), BF), V((2048, 1792), BF), V((1280, 2048), BF),
                         V((32, 8, 1792), BF), V((8, 64, 1792), BF), V((8, 8, 1792), BF),
                         V((1024, 2048), BF), V((1024, 1024), BF), V((1024, 1024), BF), V((4, 1024, 256), BF),
                         DMA((7,)), DMA((3, 3)), DMA((3, 3)), DMA((3, 3)), DMA((3, 3)), DMA((3, 7)), DMA((3, 4)),
@@ -672,7 +720,7 @@
                         DMA((1,)), DMA((1,)), DMA((2,)), DMA((2,)), DMA((2,)), DMA((2,)), DMA((4,)), DMA((4,)),
                         DMA((4, 3)), DMA((4, 3)), DMA((4, 6)), DMA((2,))],
         compiler_params=pltpu.CompilerParams(collective_id=1, has_side_effects=True, vmem_limit_bytes=VLIM),
-    )(x, dy, docs, qkv, ff, qb, fb, small, fc2, dense, cos, sin)
+    )(slots, x, dy, seg, qkv, ff, pack, fc2, dense)
 
 
 def lanes_of(shape):
@@ -692,7 +740,7 @@
     return lax.dot_general(a, b, (((0,), (0,)), ((), ())), preferred_element_type=F32)
 
 
-def attention_kernel(slot_of, a, docs, cos, sin, out, sums, seq, att, dq, dk, dv):
+def attention_kernel(slot_of, a, docs, cos, sin, out, sums, seq, flip, doc, both, dk, dv):
     def where_is(p):
         r = slot_of[p]
         ctx = lax.div(r, 2)
@@ -701,10 +749,13 @@
     for p in range(16):
         g, yy, rows = where_is(p)
         seq[64 * p : 64 * p + 64, :] = a[g, yy, 0, rows, :]
+    flip[...] = seq[...].T
+    doc[...] = jnp.broadcast_to(docs[0, 0:1, :].astype(F32), (128, 1024)).T
     dk[...] = jnp.zeros_like(dk)
     dv[...] = jnp.zeros_like(dv)
     scale = 0.125
     low = lanes_of((256, 128)) < 64
+    causal = lax.broadcasted_iota(jnp.int32, (256, 256), 0) <= lanes_of((256, 256))
     for i in range(4):
         k0 = max(0, i - 2) * 256
         kn = 256 * (i + 1) - k0
@@ -712,37 +763,35 @@
         qk, vd = seq[rq, 0:128], seq[rq, 128:256]
         kk, vv = seq[rk, 0:128], seq[rk, 128:256]
         zero = jnp.zeros((256, 128), F32)
-        qs = jnp.where(low, zero, pltpu.roll(qk.astype(F32), 64, 1)).astype(BF)
-        dsf = jnp.where(low, pltpu.roll(vd.astype(F32), 64, 1), zero)
-        s = dot_nt(qs, kk) * scale
-        qpos = 256 * i + lax.broadcasted_iota(jnp.int32, (256, kn), 0)
-        kpos = k0 + lax.broadcasted_iota(jnp.int32, (256, kn), 1)
-        own = jnp.broadcast_to(docs[0, 0:1, rq].astype(F32), (128, 256)).T[:, 0:1]
-        mask = (kpos <= qpos) & (docs[0, 0:1, rk].astype(F32) == own)
-        s = jnp.where(mask, s, NEG)
-        top = jnp.max(s, axis=-1, keepdims=True)
-        e = jnp.where(mask, jnp.exp(s - top), 0.0)
-        inv = 1.0 / jnp.sum(e, axis=-1, keepdims=True)
-        o = jnp.dot(e.astype(BF), vv, preferred_element_type=F32) * inv
-        ob = o.astype(BF)
-        att[rq, :] = ob.astype(F32)
-        delta = jnp.sum(dsf * ob.astype(F32), axis=-1, keepdims=True)
+        qs = jnp.where(low, zero, pltpu.roll(qk.astype(F32), 64, 1) * scale).astype(BF)
+        ds_lhs = jnp.where(low, pltpu.roll(vd.astype(F32), 64, 1), zero).astype(BF)
+        s = dot_nt(kk, qs)
+        same = jnp.concatenate([doc[rk, :]] * 2, axis=1) == docs[0, 0:1, rq].astype(F32)
+        last = jnp.where(same[kn - 256 :] & causal, s[kn - 256 :], NEG)
+        if kn > 256:
+            s = jnp.concatenate([jnp.where(same[: kn - 256], s[: kn - 256], NEG), last], axis=0)
+        else:
+            s = last
+        e = jnp.exp(s - jnp.max(s, axis=0, keepdims=True))
+        inv = 1.0 / jnp.sum(e, axis=0, keepdims=True)
+        o = jnp.dot(flip[128:192, rk], e.astype(BF), preferred_element_type=F32) * inv
+        delta = jnp.sum(flip[192:256, rq].astype(F32) * o.astype(BF).astype(F32), axis=0, keepdims=True)
         pr = e * inv
-        dv[rk, :] += dot_tn(pr.astype(BF), vd)
-        dp = dot_nt(dsf.astype(BF), vv)
-        ds = (pr * (dp - delta) * scale).astype(BF)
-        dq[rq, :] = jnp.dot(ds, kk, preferred_element_type=F32)
-        dk[rk, :] += dot_tn(ds, qk)
-    tot = jnp.zeros((8, 256), F32)
+        dv[rk, :] += jnp.dot(pr.astype(BF), vd, preferred_element_type=F32)
+        ds = (pr * (dot_nt(vv, ds_lhs) - delta)).astype(BF)
+        dk[rk, :] += jnp.dot(ds, qs, preferred_element_type=F32)
+        dq = jnp.dot(flip[64:128, rk], ds, preferred_element_type=F32) * scale
+        both[rq, :] = jnp.concatenate([dq, o], axis=0).T
     half = lanes_of((64, 128)) < 64
     s1 = jnp.zeros((1, 128), F32)
     s2 = jnp.zeros((1, 128), F32)
     for p in range(16):
         rows = slice(64 * p, 64 * p + 64)
         g, yy, place_rows = where_is(p)
-        t = jnp.where(half, pltpu.roll(dq[rows, :], 64, 1), pltpu.roll(dk[rows, :], 64, 1))
+        w = both[rows, :]
+        t = jnp.where(half, w, dk[rows, :])
         t = t * cos[rows, :] - partner(t) * sin[rows, :]
-        u = jnp.where(half, pltpu.roll(dv[rows, :], 64, 1), pltpu.roll(att[rows, :], 64, 1))
+        u = jnp.where(half, pltpu.roll(dv[rows, :], 64, 1), w)
         s1 += jnp.sum(t, axis=0, keepdims=True)
         s2 += jnp.sum(u, axis=0, keepdims=True)
         out[g, yy, 0, place_rows, 0:128] = t.astype(BF)
@@ -767,7 +816,7 @@
                 pl.BlockSpec((1024, 128), lambda s, t: (0, 0)),
             ],
             out_specs=(blk, pl.BlockSpec((1, 8, 256), lambda s, t: (s, 0, 0))),
-            scratch_shapes=[pltpu.VMEM((1024, 256), BF)] + [pltpu.VMEM((1024, 128), F32)] * 4,
+            scratch_shapes=[pltpu.VMEM((1024, 256), BF), pltpu.VMEM((256, 1024), BF)] + [pltpu.VMEM((1024, 128), F32)] * 4,
         ),
         out_shape=(sd((4, 2, 4, 128, 256), BF), sd((4, 8, 256), F32)),
         compiler_params=pltpu.CompilerParams(vmem_limit_bytes=VLIM),
@@ -1183,8 +1232,8 @@
     )(att, normed, dy, x, act, dup, wc, w2, sums, dsum)
 
 
-def finish_kernel(x, dy, yo, o1, o2, cst, y, dx, dqkv, dff, dfc2, ddense):
-    low = lanes_of((64, 128)) < 64
+def finish_kernel(x, dy, yo, o1, o2a, o2b, cst, y, dx, dqkv, dff, dfc2, ddense):
+    low = lanes_of((16, 128)) < 64
     for i in range(16):
         yy, g, zp = i // 8, (i // 2) % 4, i % 2
         a, b = yy * 4 + 2 * zp, yy * 4 + 2 * zp + 1
@@ -1203,11 +1252,10 @@
     for h in range(32):
         mm, g = (h // 16) * 4 + h % 4, (h // 4) % 4
         dff[:, 256 * h : 256 * h + 256] = o1[mm, :, 768 + 256 * g : 1024 + 256 * g].astype(F32)
-    dfc2[...] = o2[0:256, :].astype(F32)
-    ddense[...] = o2[256:320, :].astype(F32)
-
-    def body(i, carry):
-        sl = pl.ds(pl.multiple_of(16 * i, 16), 16)
+    dfc2[...] = o2a[...].astype(F32)
+    ddense[...] = o2b[...].astype(F32)
+    for i in range(2):
+        sl = slice(16 * i, 16 * i + 16)
         xf = x[sl, :].astype(F32)
         cen = xf - jnp.mean(xf, axis=-1, keepdims=True)
         rstd = lax.rsqrt(jnp.mean(cen * cen, axis=-1, keepdims=True) + EPS)
@@ -1217,22 +1265,32 @@
         dx[sl, :] = dy[sl, :].astype(F32) + rstd * (
             gr - jnp.mean(gr, axis=-1, keepdims=True) - xhat * jnp.mean(gr * xhat, axis=-1, keepdims=True)
         )
-        return carry
-
-    lax.fori_loop(0, 8, body, 0)
 
 
 def finish_all(x, dy, yo, o1, o2, cst):
     sd = jax.ShapeDtypeStruct
+
+    def rows(count, width, first=0):
+        return pl.BlockSpec((count, width), lambda i: (first + i, 0))
+
     return pl.pallas_call(
         finish_kernel,
         name="finish_all",
+        grid=(4,),
         out_shape=(sd((128, 2048), BF), sd((128, 2048), F32), sd((64, 6144), F32), sd((64, 8192), F32),
                    sd((256, 2048), F32), sd((64, 2048), F32)),
-        in_specs=[VM] * 6,
-        out_specs=(VM,) * 6,
+        in_specs=[
+            rows(32, 2048),
+            rows(32, 2048),
+            pl.BlockSpec((2, 32, 2048), lambda i: (0, i, 0)),
+            pl.BlockSpec((8, 16, 1792), lambda i: (0, i, 0)),
+            rows(64, 2048),
+            rows(16, 2048, 16),
+            pl.BlockSpec((8, 2048), lambda i: (0, 0)),
+        ],
+        out_specs=(rows(32, 2048), rows(32, 2048), rows(16, 6144), rows(16, 8192), rows(64, 2048), rows(16, 2048)),
         compiler_params=pltpu.CompilerParams(vmem_limit_bytes=VLIM),
-    )(x, dy, yo, o1, o2, cst)
+    )(x, dy, yo, o1, o2, o2, cst)
 
 
 def stored_columns(a):
@@ -1241,15 +1299,6 @@
     v = a[:, :, 512:768].reshape(2, 4, rows, 4, 64).transpose(2, 0, 3, 1, 4).reshape(rows, 1, 2048)
     f = a[:, :, 768:1792].reshape(2, 4, rows, 4, 256).transpose(2, 0, 3, 1, 4).reshape(rows, 8192)
     return jnp.concatenate([qk, v], axis=1).reshape(rows, 6144), f
-
-
-def rotary_lanes(pos):
-    lane = jnp.arange(128, dtype=jnp.int32) % 64
-    freqs = jnp.exp(-(2.0 * (lane % (ROT // 2)).astype(F32) / ROT) * math.log(10000.0))
-    angles = pos.astype(F32)[:, None] * freqs[None]
-    turns = lane < ROT
-    sign = jnp.where(turns, jnp.where(lane < ROT // 2, -1.0, 1.0), 0.0)
-    return jnp.where(turns, jnp.cos(angles), 1.0), jnp.sin(angles) * sign
 
 
 def fast_device(
@@ -1260,23 +1309,10 @@
     index = ctx * 4 + z
     xb, dyb = block_input[0], output_grad[0]
 
-    def spread(piece, total):
-        count = piece.shape[0]
-        own = jnp.arange(total, dtype=jnp.int32) // count == index
-        return jnp.where(own, jnp.tile(piece, total // count), jnp.zeros((), BF))
-
-    docs = jnp.broadcast_to(segment.astype(BF), (8, 1024))
-    qb = jnp.broadcast_to(spread(qkv_b, 6144)[None], (8, 6144))
-    fb = jnp.broadcast_to(spread(fc1_b, 8192)[None], (8, 8192))
-    vecs = jnp.stack([spread(v, 2048) for v in (ln_gain, ln_bias, dense_b, fc2_b)])
-    rest = jnp.pad(vecs[:, 1792:].reshape(1, 1024), ((0, 0), (0, 768)))
-    small = jnp.concatenate([jnp.zeros((1, 1792), BF), vecs[:, :1792], rest, jnp.zeros((2, 1792), BF)], axis=0)
-    pairs = lax.dynamic_slice_in_dim(slots.reshape(2, 4, 2), g, 1, 1).reshape(4)
-    rows = (pairs[:, None] * 64 + jnp.arange(64, dtype=jnp.int32)[None]).reshape(256)
-    cos2, sin2 = rotary_lanes(rows)
-    cos, sin = rotary_lanes(jnp.arange(1024, dtype=jnp.int32))
-    xg, dg, docg, normed, act, dup, wc, w2g, heads, dsum, cst = gather_all(
-        xb, dyb, docs, qkv_w, fc1_w, qb, fb, small, fc2_w, dense_w, cos2, sin2
+    vecs = [jnp.pad(v, (0, 256 - v.shape[0])) for v in (ln_gain, ln_bias, dense_b, fc2_b, qkv_b, fc1_b)]
+    pack = jnp.stack(vecs + [jnp.zeros_like(fc1_b)] * 2)
+    xg, dg, docg, normed, act, dup, wc, w2g, heads, dsum, cst, cos, sin = gather_all(
+        slots, xb, dyb, segment, qkv_w, fc1_w, pack, fc2_w, dense_w
     )
     slot_of = jnp.sum(jnp.where(slots[None, :] == jnp.arange(16, dtype=jnp.int32)[:, None], jnp.arange(16, dtype=jnp.int32)[None, :], 0), axis=1)
     att, sums = attention(slot_of, heads.reshape(4, 2, 4, 128, 256), docg, cos, sin)

time: 340 us -> 323 us (0.950)
  Pallas kernels: 318 us -> 309 us
  other arithmetic: 6.65 us -> 0.66 us
    pallas_call x1, Pallas kernels: 24.3 us -> 16.9 us  [attention(): pl.pallas_call(attention_kernel, name='attention', grid_spec=pltpu.Prefet...]
    mul x3 -> x0, other arithmetic: 4.35 us -> none  [the longest x2 4.33 us: rotary_lanes(): return (jnp.where(turns, jnp.cos(angles), 1.0), jnp.sin(angles) * sign)]
where the time goes in v1:
time: 323 us; the launch traced here: 320 us
  Pallas kernels  309 us (96%)
  local copies, waits for them, and re-layouts  9.25 us (3%)
    pallas_call x1, Pallas kernels, reduce_all(): pl.pallas_call(reduce_kernel, name='reduce_all', out_shape=(sd((2, 128, 2...  151 us
    pallas_call x1, Pallas kernels, gather_all(): pl.pallas_call(gather_kernel, name='gather_all', out_shape=(sd((1024, 204...  134 us
    pallas_call x1, Pallas kernels, attention(): pl.pallas_call(attention_kernel, name='attention', grid_spec=pltpu.Prefet...  16.9 us
    pallas_call x1, Pallas kernels, finish_all(): pl.pallas_call(finish_kernel, name='finish_all', grid=(4,), out_shape=(sd...  6.61 us

profile of v1, /device:TPU:8, one launch (start us, length us, event | category | flops | bytes accessed | tf_op | source)
XLA Modules:
  0.0 319.5 jit_solution(7160325444195107015)
XLA Ops:
  0.6 0.7 pad.17
  1.3 0.7 pad.18
  2.0 0.7 pad.19
  2.6 0.7 pad.20
  3.3 0.7 pad.21
  4.0 0.7 stack.29
  4.6 0.6 stack.31.pack
  5.3 134.5 %gather_all.1 = (bf16[1024,2048]{1,0:T(8,128)(2,1)}, bf16[1024,2048]{1,0:T(8,128)(2,1)}, bf16[8,8,1024]{2,1,0:T(8,128)(2,1)}, bf16[1024,2048]{1,0:T(8,128)(2,1)}...) custom-call(s32[16]{0:T(128)} %slots.1, ...), custom_call_target="tpu_custom_call" | custom-call | tf_op jit(solution)/shard_map/gather_all/pallas_call | solution.py:706
  139.8 0.6 select_reduce_fusion.slot_of
  140.4 16.9 %attention.1 = (bf16[4,2,4,128,256]{4,3,2,1,0:T(8,128)(2,1)}, f32[4,8,256]{2,1,0:T(8,128)}) custom-call(s32[16]{0:T(128)} %select_reduce_fusion.slot_of, bf16[4,2,4,128,256]{4,3,2,1,0:T(8,128)(2,1)} %bitcast.29, bf16[8,8,1024]{2,1,0:T(8,128)(2,1)} %get-tuple-element.39.docs, f32[1024,128]{1,0:T(8,128)} %get-tuple-element.40.cos, ...), custom_call_target="tpu_custom_call" | custom-call | tf_op jit(solution)/shard_map/attention/pallas_call | solution.py:806
  157.3 150.8 %reduce_all.1 = (f32[2,128,2048]{2,1,0:T(8,128)}, bf16[8,64,1792]{2,1,0:T(8,128)(2,1)}, bf16[320,2048]{1,0:T(8,128)(2,1)}, f32[8,16,128]{2,1,0:T(8,128)}, f32[8,2048]{1,0:T(8,128)}) custom-call(bf16[4,1024,256]{2,1,0:T(8,128)(2,1)} %bitcast.34, bf16[1024,2048]{1,0:T(8,128)(2,1)} %get-tuple-element.43.normed_i, bf16[1024,2048]{1,0:T(8,128)(2,1)} %get-tuple-element.44.dy_i, ...), custom_call_target="tpu_custom_call" | custom-call | tf_op jit(solution)/shard_map/reduce_all/pallas_call | solution.py:1210
  308.2 0.9 copy.35
  309.1 0.1 reshape.55
  309.2 0.1 reshape.56
  309.3 0.1 reshape.57
  309.4 0.1 reshape.58
  309.5 0.6 dynamic_slice.15
  310.1 6.6 %finish_all.1 = (bf16[128,2048]{1,0:T(8,128)(2,1)}, f32[128,2048]{1,0:T(8,128)}, f32[64,6144]{1,0:T(8,128)}, f32[64,8192]{1,0:T(8,128)}, f32[256,2048]{1,0:T(8,128)}, /*index=5*/f32[64,2048]{1,0:T(8,128)}) custom-call(bf16[128,2048]{1,0:T(8,128)(2,1)} %bitcast.31, bf16[128,2048]{1,0:T(8,128)(2,1)} %bitcast.33, f32[2,128,2048]{2,1,0:T(8,128)} %get-tuple-element.52.yo, ...), custom_call_target="tpu_custom_call" | custom-call | tf_op jit(solution)/shard_map/finish_all/pallas_call | solution.py:1276
  316.8 0.1 reduce_sum.22
  316.9 0.5 fusion
  317.5 0.6 dynamic_slice.18
  318.1 0.8 slice.30
  318.9 0.1 fusion.1
  319.0 0.5 copy.37
  (22 shorter events, 0.2 us)
Async XLA Ops:
  5.3 134.5 %copy-start = (s32[16]{0:T(128)S(1)}, s32[16]{0:T(128)}, u32[]{:S(2)}) copy-start(s32[16]{0:T(128)} %slots.1) | copy-start | bytes 196
  319.0 0.5 copy-start.1
